TPU v7x, 32 devices: a whole 2x2x4 slice. The times are simulated.
32 devices in a mesh: dp: 8 (over z, y), grp: 4 (over x, core).
Axes of the slice: x: 2, y: 2, z: 4, core: 2. Of those that a mesh axis runs over, the one named last changes fastest.
Arguments:
- quot_ids: int32 [4096, 2], P(('dp', 'grp')), may hold values from 0 to 127
- rem_ids: int32 [4096, 2], P(('dp', 'grp')), may hold values from 0 to 16383, as said below
- labels: int32 [4096], P(('dp', 'grp')), may hold values 0 or 1
- quot_table: bfloat16 [2, 128, 512], replicated, may hold values from -6 to 6
- rem_table: bfloat16 [2, 16384, 512], P(None, 'grp'), may hold values from -6 to 6
- w1: bfloat16 [1024, 512], replicated, may hold values from -0.1875 to 0.1875
- b1: float32 [512], replicated, may hold values from -3 to 3
- w2: bfloat16 [512], replicated, may hold values from -0.5 to 0.5
- b2: float32 [1], replicated, may hold values from -3 to 3
Outputs:
- losses: float32 [4096], P(('dp', 'grp'))
- grad_rem: float32 [2, 16384, 512], P(None, 'grp', 'dp')
- grad_quot: float32 [2, 128, 512], replicated
- grad_w1: float32 [1024, 512], replicated
- grad_b1: float32 [512], replicated
- grad_w2: float32 [512], replicated
- grad_b2: float32 [1], replicated
Inputs may be any that keep to these rules, and one draw needn't show every extreme that they name: `rem_ids`: in each aligned block of 128 samples and each feature, at most 64 remainder indices r share the same r // 4096, and exactly 64 do for some value of r // 4096.
All inputs are finite; a program needn't handle non-finite values. No bound on the sum of `labels` on one device may be relied on, other than what follows from the above.
Results may differ from a plain program's by a relative error of at most 0.0051.
Values may be sent and summed in bfloat16 or wider, within the bound.
No kernel may reach another device: no remote copies, remote signals or barrier semaphores. Data moves between devices by JAX's collectives and lax.ppermute only.
A program may use at most 128 MiB of HBM per device.

v0:
```python
import jax
import jax.numpy as jnp
from jax import lax
from jax.sharding import PartitionSpec as P


def scatter_rows(shard_grad, positions, values):
    for feature in range(shard_grad.shape[0]):
        shard_grad = shard_grad.at[feature, positions[:, feature]].add(
            values[:, feature].astype(jnp.float32), mode="drop"
        )
    return shard_grad


def pick_rows(rem_table, wanted, filled):
    pieces = []
    for feature in range(rem_table.shape[0]):
        picked = jnp.take(rem_table[feature], wanted[:, feature], axis=0)
        pieces.append(jnp.where(filled[:, feature : feature + 1], picked, jnp.zeros_like(picked)))
    return jnp.concatenate(pieces, axis=1)


def on_device(quot_ids, rem_ids, labels, quot_table, rem_table, w1, b1, w2, b2):
    features = rem_ids.shape[1]
    shard_rows = rem_table.shape[1]
    model_width = rem_table.shape[2]
    table_rows = quot_table.shape[1]
    owner_index = lax.axis_index("grp")
    gathered_ids = lax.all_gather(rem_ids, "grp", axis=0, tiled=True)
    local_rows = gathered_ids - owner_index * shard_rows
    inside = (local_rows >= 0) & (local_rows < shard_rows)
    safe_rows = jnp.clip(local_rows, 0, shard_rows - 1)
    partial_value = pick_rows(rem_table, safe_rows, inside).astype(jnp.float32)
    rem_rows = lax.psum_scatter(
        partial_value.astype(jnp.bfloat16), "grp", scatter_dimension=0, tiled=True
    )
    quot_parts = []
    onehots = []
    for feature in range(features):
        onehot = (
            quot_ids[:, feature][:, None] == jnp.arange(table_rows, dtype=jnp.int32)[None, :]
        ).astype(jnp.bfloat16)
        onehots.append(onehot)
        quot_parts.append(jnp.dot(onehot, quot_table[feature], preferred_element_type=jnp.float32))
    quot_rows = jnp.concatenate(quot_parts, axis=1)
    rem_float = rem_rows.astype(jnp.float32)
    joined = (quot_rows * rem_float).astype(jnp.bfloat16)
    preact = jnp.dot(joined, w1, preferred_element_type=jnp.float32) + b1
    hidden = jax.nn.silu(preact).astype(jnp.bfloat16)
    logits = jnp.dot(hidden, w2, preferred_element_type=jnp.float32) + b2[0]
    target = labels.astype(jnp.float32)
    losses = jax.nn.softplus(logits) - target * logits
    dlogits = jax.nn.sigmoid(logits) - target
    grad_b2 = jnp.sum(dlogits)[None]
    grad_w2 = jnp.dot(dlogits, hidden.astype(jnp.float32), precision=lax.Precision.HIGHEST)
    sigmoid_pre = jax.nn.sigmoid(preact)
    slopes = sigmoid_pre * (1.0 + preact * (1.0 - sigmoid_pre))
    dpreact = dlogits[:, None] * w2.astype(jnp.float32)[None, :] * slopes
    grad_b1 = jnp.sum(dpreact, axis=0)
    rounded = dpreact.astype(jnp.bfloat16)
    grad_w1 = jnp.dot(joined.T, rounded, preferred_element_type=jnp.float32)
    djoined = jnp.dot(rounded, w1.T, preferred_element_type=jnp.float32)
    rem_grads = (djoined * quot_rows).astype(jnp.bfloat16)
    quot_grads = djoined * rem_float
    quot_list = []
    for feature in range(features):
        quot_list.append(
            jnp.dot(
                onehots[feature].astype(jnp.float32).T,
                quot_grads[:, feature * model_width : (feature + 1) * model_width],
                precision=lax.Precision.HIGHEST,
            )
        )
    grad_quot = jnp.stack(quot_list, axis=0)
    grad_w1, grad_b1, grad_w2, grad_b2, grad_quot = lax.psum(
        (grad_w1, grad_b1, grad_w2, grad_b2, grad_quot), ("dp", "grp")
    )
    group_rows = lax.all_gather(rem_grads, "grp", axis=0, tiled=True)
    group_rows = group_rows.reshape(group_rows.shape[0], features, model_width)
    positions = jnp.where(inside, local_rows, shard_rows)
    received = lax.all_to_all(group_rows, "dp", split_axis=2, concat_axis=0, tiled=True)
    all_positions = lax.all_gather(positions, "dp", axis=0, tiled=True)
    shard_grad = jnp.zeros((features, shard_rows, received.shape[2]), jnp.float32)
    grad_rem = scatter_rows(shard_grad, all_positions, received)
    return (losses, grad_rem, grad_quot, grad_w1, grad_b1, grad_w2, grad_b2)


def solution(mesh):
    placed = (
        P(("dp", "grp"), None),
        P(("dp", "grp"), None),
        P(("dp", "grp")),
        P(),
        P(None, "grp", None),
        P(),
        P(),
        P(),
        P(),
    )
    return jax.shard_map(
        on_device,
        mesh=mesh,
        in_specs=placed,
        out_specs=(P(("dp", "grp")), P(None, "grp", "dp"), P(), P(), P(), P(), P()),
        check_vma=False,
    )
```

profile of v0, /device:TPU:0, one launch (start us, length us, event | category | flops | bytes accessed | tf_op | source)
XLA Modules:
  0.0 262.6 jit_solution(8166397708621926012)
XLA Ops:
  7.2 0.0 copy-start
  7.2 0.0 reduce-scatter.2.cloned.1.call-start
  7.2 6.4 %all_gather.9 = s32[512,2]{0,1:T(2,128)S(1)} all-gather(s32[128,2]{0,1:T(2,128)} %param.12), channel_id=1, replica_groups=mesh['dp'=8,'grp'=4] {'grp'}, dimensions={0}, use_global_device_ids=true | all-gather | bytes 5120 | tf_op jit(solution)/shard_map/all_gather | solution.py:29
  13.7 5.7 %slice_bitcast_fusion.1 = (bf16[4096,512]{1,0:T(8,128)(2,1)}, bf16[4096,512]{1,0:T(8,128)(2,1)}) fusion(bf16[2,4096,512]{2,1,0:T(8,128)(2,1)} %param.15), kind=kLoop, calls=%fused_computation.5 | loop fusion | bytes 16777216 | tf_op jit(solution)/shard_map/squeeze | solution.py:18
  19.5 4.7 %gather_fusion.1 = bf16[512,512]{1,0:T(8,128)(2,1)S(1)} fusion(bf16[4096,512]{1,0:T(8,128)(2,1)} %get-tuple-element.43, s32[1024]{0:T(1024)S(1)} %pad_clamp_fusion), kind=kCustom, calls=%fused_computation.1.clone | custom fusion | bytes 1050624 | tf_op jit(solution)/shard_map/jit(_take)/gather | solution.py:18
  24.2 0.0 copy-start.6
  24.3 0.0 copy-start.7
  24.3 0.0 copy-start.1
  24.3 4.8 %gather_fusion = bf16[512,512]{1,0:T(8,128)(2,1)S(1)} fusion(bf16[4096,512]{1,0:T(8,128)(2,1)} %get-tuple-element.42, s32[1024]{0:T(1024)S(1)} %pad_clamp_fusion.1), kind=kCustom, calls=%fused_computation.clone | custom fusion | bytes 1050624 | tf_op jit(solution)/shard_map/jit(_take)/gather | solution.py:18
  29.0 0.0 copy-start.11
  29.1 0.0 copy-start.8
  29.1 0.6 select_select_fusion
  29.6 1.1 pad_maximum_fusion
  30.7 0.0 reduce-scatter.2.cloned.1.call-update
  30.8 0.0 all-gather.2.cloned.1.call-start
  30.8 0.0 copy-done.6
  30.8 0.0 copy-start.2
  31.5 0.0 copy-done.7
  31.5 0.0 copy-start.5
  31.5 0.0 copy-start.4
  31.6 0.0 copy-done.1
  31.6 0.2 fusion.8
  31.8 0.3 copy-done.5
  32.0 0.2 fusion.10
  32.3 25.1 %reduce-scatter.2.cloned.1.call-done = bf16[128,1024]{1,0:T(8,128)(2,1)} async-done(((bf16[512,1024]{1,0:T(8,128)(2,1)}), bf16[128,1024]{1,0:T(8,128)(2,1)}) %reduce-scatter.2.cloned.1.call-update) | async-done | bytes 262160 | tf_op jit(solution)/shard_map/reduce_scatter | solution.py:34
  57.4 0.0 copy-done
  57.4 0.0 copy-done.11
  57.4 1.3 multiply_convert_fusion.1
  58.7 0.0 copy-done.8
  58.7 1.3 fusion.30
  60.0 2.2 convert_multiply_fusion
  62.2 0.0 all-gather.2.cloned.1.call-update
  62.2 32.3 %all_gather.10 = s32[4096,2]{0,1:T(2,128)} all-gather(s32[512,2]{0,1:T(2,128)S(1)} %get-tuple-element.50), channel_id=1, replica_groups=mesh['dp'=8,'grp'=4] {'dp'}, dimensions={0}, use_global_device_ids=true | all-gather | bytes 36864 | tf_op jit(solution)/shard_map/all_gather | solution.py:82
  94.5 0.0 all-gather.2.cloned.1.call-done
  94.5 1.8 reshape.29
  96.4 3.8 %copy.25 = bf16[512,2,512]{0,1,2:T(2,128)(2,1)} copy(bf16[512,2,512]{2,1,0:T(2,128)(2,1)S(1)} %reshape.29) | data formatting | bytes 2097152 | tf_op jit(solution)/shard_map/reshape | solution.py:79
  100.1 5.4 %all-to-all-start = ((bf16[512,2,512]{0,1,2:T(2,128)(2,1)}), bf16[512,2,512]{0,1,2:T(2,128)(2,1)S(1)}, u32[]{:S(2)}, u32[]{:S(2)}) async-start(bf16[512,2,512]{0,1,2:T(2,128)(2,1)} %copy.25), calls=%async_computation.1 | async-start | bytes 2097152 | tf_op jit(solution)/shard_map/all_to_all | solution.py:81
  105.5 0.0 all-reduce.6.cloned.1.call-start
  105.6 0.9 compare_select_fusion.1
  106.4 0.0 copy-done.9
  106.4 0.1 fusion.19
  106.6 0.0 copy-done.10
  106.6 0.2 and_reduce_fusion
  106.8 0.6 broadcast_select_fusion
  107.4 1.0 convolution_bitcast_fusion
  108.5 1.0 convolution_bitcast_fusion.1
  109.5 0.8 pad_maximum_fusion.2
  110.3 2.8 %fusion.14 = f32[1024,512]{1,0:T(8,128)} fusion(bf16[128,1024]{1,0:T(8,128)(2,1)} %reduce-scatter.2.cloned.1.call-done, f32[128,512]{1,0:T(8,128)S(1)} %fusion.8, f32[128,512]{1,0:T(8,128)S(1)} %fusion.10, f32[128,512]{1,0:T(8,128)S(1)} %get-tuple-element.58, f32[512]{0:T(512)} %copy-done.2, f32[128]{0:T(128)} %copy-done.3), kind=kOutput, calls=%fused_computation.39 | convolution fusion | flops 135397376 | bytes 3148288 | tf_op jit(solution)/shard_map/dot_general | solution.py:61
  113.1 0.0 all-reduce.6.cloned.1.call-update
  113.2 0.8 fusion.29
  114.0 0.8 fusion.25
  114.8 40.5 %all-reduce.2 = (f32[512]{0:T(512)}, f32[512]{0:T(512)}, f32[1]{0:T(128)}) all-reduce(f32[512]{0:T(512)S(1)} %fusion.29, f32[512]{0:T(512)S(1)} %bitcast.59, f32[1]{0:T(128)} %bitcast.19), channel_id=1, replica_groups=mesh['dp'=8,'grp'=4] {'dp','grp'}, use_global_device_ids=true, to_apply=%region_6.8 | all-reduce | flops 1025 | bytes 8200 | tf_op jit(solution)/shard_map/psum | solution.py:75
  155.3 0.0 all-to-all-done
  155.3 0.2 copy.26
  155.5 0.1 copy.34
  155.6 1.2 fusion.4
  156.8 1.9 copy.28
  158.7 1.8 copy.29
  160.5 24.8 %scatter_custom_fusion = f32[8192,64]{1,0:T(8,128)} fusion(s32[4096]{0:T(1024)} %get-tuple-element.62, f32[4096,64]{1,0:T(8,128)} %copy.28, f32[]{:T(128)} %constant.3.clone.1), kind=kCustom, calls=%fused_computation.6 | custom fusion | flops 262144 | bytes 2097664
  185.4 24.2 %scatter_fusion = f32[8192,64]{1,0:T(8,128)} fusion(f32[8192,64]{1,0:T(8,128)} %scatter_custom_fusion, s32[4096]{0:T(1024)S(1)} %get-tuple-element.61, f32[4096,64]{1,0:T(8,128)S(1)} %copy.29), kind=kCustom, calls=%fused_computation.3 | custom fusion | flops 262144 | bytes 3162112
  209.6 3.8 %copy.31 = f32[2,4096,64]{1,2,0:T(8,128)} copy(f32[2,4096,64]{2,1,0:T(8,128)} %bitcast.52) | data formatting | bytes 4194304
  213.4 37.7 %all-reduce.6.cloned.1.call-done = (f32[2,128,512]{2,1,0:T(8,128)}, f32[1024,512]{1,0:T(8,128)}) async-done(((f32[2,128,512]{2,1,0:T(8,128)}, f32[1024,512]{1,0:T(8,128)}), (f32[2,128,512]{2,1,0:T(8,128)}, f32[1024,512]{1,0:T(8,128)})) %all-reduce.6.cloned.1.call-update) | async-done | bytes 2621456 | tf_op jit(solution)/shard_map/psum | solution.py:75
  251.1 1.9 copy.39
  253.0 3.1 %copy.40 = f32[1024,512]{1,0:T(8,128)} copy(f32[1024,512]{1,0:T(8,128)} %get-tuple-element.66) | data formatting | bytes 4194304
  (19 shorter events, 0.1 us)
Async XLA Ops:
  7.2 50.3 %copy-start = (bf16[1024,512]{1,0:T(8,128)(2,1)S(1)}, bf16[1024,512]{1,0:T(8,128)(2,1)}, u32[]{:S(2)}) copy-start(bf16[1024,512]{1,0:T(8,128)(2,1)} %param.16) | copy-start | bytes 3145732
  7.2 50.2 %reduce-scatter.2.cloned.1.call-start = ((), (), s32[]{:S(2)}) async-start(), calls=%async_computation.2 | async-start | bytes 1310720 | tf_op jit(solution)/shard_map/reduce_scatter | solution.py:34
  24.2 6.6 %copy-start.6 = (bf16[512]{0:T(512)(128)(2,1)S(1)}, bf16[512]{0:T(512)(128)(2,1)}, u32[]{:S(2)}) copy-start(bf16[512]{0:T(512)(128)(2,1)} %param.18) | copy-start | bytes 3076
  24.3 7.3 %copy-start.7 = (s32[128,2]{0,1:T(2,128)S(1)}, s32[128,2]{0,1:T(2,128)}, u32[]{:S(2)}) copy-start(s32[128,2]{0,1:T(2,128)} %param.11) | copy-start | bytes 3076
  24.3 7.3 %copy-start.1 = (bf16[2,128,512]{2,1,0:T(8,128)(2,1)S(1)}, bf16[2,128,512]{2,1,0:T(8,128)(2,1)}, u32[]{:S(2)}) copy-start(bf16[2,128,512]{2,1,0:T(8,128)(2,1)} %param.14) | copy-start | bytes 786436
  29.0 28.4 %copy-start.11 = (f32[512]{0:T(512)S(1)}, f32[512]{0:T(512)}, u32[]{:S(2)}) copy-start(f32[512]{0:T(512)} %param.17) | copy-start | bytes 6148
  29.1 29.7 %copy-start.8 = (s32[128]{0:T(128)S(1)}, s32[128]{0:T(128)}, u32[]{:S(2)}) copy-start(s32[128]{0:T(128)} %param.13) | copy-start | bytes 1540
  30.8 63.7 %all-gather.2.cloned.1.call-start = ((), (), s32[]{:S(2)}) async-start(), calls=%async_computation.3 | async-start | bytes 1310720 | tf_op jit(solution)/shard_map/all_gather | solution.py:78
  30.8 63.6 %copy-start.2 = (f32[512]{0:T(512)}, f32[512]{0:T(512)S(1)}, u32[]{:S(2)}) copy-start(f32[512]{0:T(512)S(1)} %convert_element_type.44) | copy-start | bytes 6148
  31.5 0.5 copy-start.5
  31.5 28.5 %copy-start.4 = (s32[128]{0:T(128)}, s32[128]{0:T(128)S(1)}, u32[]{:S(2)}) copy-start(s32[128]{0:T(128)S(1)} %get-tuple-element.55) | copy-start | bytes 1540
  60.0 34.5 %copy-start.3 = (f32[128]{0:T(128)}, f32[128]{0:T(128)S(1)}, u32[]{:S(2)}) copy-start(f32[128]{0:T(128)S(1)} %get-tuple-element.41) | copy-start | bytes 1540
  60.0 46.4 %copy-start.9 = (s32[2]{0:T(128)S(1)}, s32[2]{0:T(128)}, u32[]{:S(2)}) copy-start(s32[2]{0:T(128)} %constant.13) | copy-start | bytes 28
  60.0 46.6 %copy-start.10 = (s32[2]{0:T(128)S(1)}, s32[2]{0:T(128)}, u32[]{:S(2)}) copy-start(s32[2]{0:T(128)} %constant.28) | copy-start | bytes 28
  100.1 55.2 %all-to-all-start = ((bf16[512,2,512]{0,1,2:T(2,128)(2,1)}), bf16[512,2,512]{0,1,2:T(2,128)(2,1)S(1)}, u32[]{:S(2)}, u32[]{:S(2)}) async-start(bf16[512,2,512]{0,1,2:T(2,128)(2,1)} %copy.25), calls=%async_computation.1 | async-start | bytes 2097152 | tf_op jit(solution)/shard_map/all_to_all | solution.py:81
  105.5 145.6 %all-reduce.6.cloned.1.call-start = ((), (), s32[]{:S(2)}) async-start(), calls=%async_computation.4 | async-start | bytes 5242880 | tf_op jit(solution)/shard_map/psum | solution.py:75
Sparse Core Ops, SparseCore 0:
  30.9 26.4 reduce-scatter.1
  62.3 16.6 all-gather.1
  113.3 137.7 all-reduce.5
where the time goes:
time: 263 us
  blocking collectives  79.2 us (30%)
  waiting for transfers between devices  62.9 us (24%)
  other arithmetic  55.4 us (21%)
  local copies, waits for them, and re-layouts  33.9 us (13%)
  between operations  14.7 us (6%)
  matrix products  10.9 us (4%)
  starting transfers between devices  5.49 us (2%)
    unnamed x5, other arithmetic  50 us
    psum x1, blocking collectives, on_device(): lax.psum((grad_w1, grad_b1, grad_w2, grad_b2, grad_quot), ('dp', 'grp'))  40.5 us
    psum x1, waiting for transfers between devices, on_device(): lax.psum((grad_w1, grad_b1, grad_w2, grad_b2, grad_quot), ('dp', 'grp'))  37.7 us
    all_gather x1, blocking collectives, on_device(): all_positions = lax.all_gather(positions, 'dp', axis=0, tiled=True)  32.3 us
    reduce_scatter x1, waiting for transfers between devices, on_device(): lax.psum_scatter(partial_value.astype(jnp.bfloat16), 'grp', scatter_dimen...  25.1 us
    gather x2, local copies, waits for them, and re-layouts, pick_rows(): picked = jnp.take(rem_table[feature], wanted[:, feature], axis=0)  9.47 us
    unnamed x28, local copies, waits for them, and re-layouts  9.05 us
    all_gather x1, blocking collectives, on_device(): gathered_ids = lax.all_gather(rem_ids, 'grp', axis=0, tiled=True)  6.42 us
  transfers between devices with their start and end apart: 4, of which 2 were waited for; matrix products, arithmetic and copies ran while one was open for 26% of the time, Pallas kernels for 0%

commit v1 on v0

v1 whole, which is shorter than its diff:
```python
import functools

import jax
import jax.numpy as jnp
from jax import lax
from jax.experimental import pallas as pl
from jax.experimental.pallas import tpu as pltpu
from jax.sharding import Mesh, PartitionSpec as P


f32 = jnp.float32
bf16 = jnp.bfloat16
VM = pl.BlockSpec(memory_space=pltpu.VMEM)
SM = pl.BlockSpec(memory_space=pltpu.SMEM)
TINY = 8
HIGH = 256


def iota(shape, dim):
    return lax.broadcasted_iota(jnp.int32, shape, dim)


def mm(a, b, dims=((1,), (0,)), **kw):
    return lax.dot_general(a, b, (dims, ((), ())), preferred_element_type=f32, **kw)


def call(body, outs, args, in_specs, scratch=()):
    multi = isinstance(outs, (tuple, list))
    return pl.pallas_call(
        body,
        out_shape=outs,
        in_specs=in_specs,
        out_specs=tuple(VM for _ in outs) if multi else VM,
        scratch_shapes=list(scratch),
    )(*args)


def tree_sum(parts):
    parts = list(parts)
    while len(parts) > 1:
        parts = [a + b for a, b in zip(parts[::2], parts[1::2])]
    return parts[0]


def pack_tiny(b1_row, w2_row, b2_row):
    width = b1_row.shape[1]
    which = iota((TINY, width), 0)
    out = jnp.zeros((TINY, width), f32)
    at = 0
    for row in (b1_row, w2_row, b2_row):
        rest = row
        for _ in range(3):
            head = rest.astype(bf16).astype(f32)
            if at < TINY:
                out = jnp.where(which == at, head, out)
            rest = rest - head
            at += 1
        if at == 6:
            break
    lane = iota((1, width), 1)
    rest = b2_row
    last = jnp.zeros((1, width), f32)
    for piece in range(3):
        head = rest.astype(bf16).astype(f32)
        last = jnp.where(lane == piece, head, last)
        rest = rest - head
    out = jnp.where(which == 6, last, out)
    return out.astype(bf16)


def unpack_tiny(block):
    block = block.astype(f32)
    b1_row = block[0:1] + block[1:2] + block[2:3]
    w2_row = block[3:4] + block[4:5] + block[5:6]
    b2_row = block[6:7, 0:1] + block[6:7, 1:2] + block[6:7, 2:3]
    return b1_row, w2_row, jnp.broadcast_to(b2_row, b1_row.shape)


def fetch_body(me_ref, ids_ref, table_ref, out_ref, *, cap):
    n_rows, tok = ids_ref.shape
    feats, shard, _ = table_ref.shape
    groups = n_rows // feats
    local = ids_ref[...] - me_ref[0] * shard
    mine = (local >= 0) & (local < shard)
    before = (iota((tok, tok), 0) < iota((tok, tok), 1)).astype(f32)
    key = jnp.where(mine, mm(mine.astype(f32), before), -1.0).astype(jnp.int32)
    value = local.astype(f32)
    slot = iota((cap, tok), 0)
    for f in range(feats):
        cols = []
        for k in range(groups):
            at = slice(k * feats + f, k * feats + f + 1)
            hit = jnp.where(key[at, :] == slot, value[at, :], 0.0)
            cols.append(jnp.sum(hit, axis=1, keepdims=True))
        col = jnp.concatenate(cols, axis=0).astype(jnp.int32)
        hot = (col == iota((groups * cap, shard), 1)).astype(f32).astype(bf16)
        got = mm(hot, table_ref[f]).astype(bf16)
        out_ref[:, f * cap : (f + 1) * cap, :] = got.reshape(groups, cap, got.shape[1])


def slots_body(rem_ref, quot_ref, label_ref, table_ref, pick_ref, q_ref, cols_ref, code_ref, *, shard, cap, groups, high):
    feats, tok = rem_ref.shape
    width = table_ref.shape[2]
    pad = jnp.zeros((8 - 2 * feats - 1, tok), f32)
    cols = jnp.concatenate(
        [rem_ref[...].astype(f32), quot_ref[...].astype(f32), label_ref[...].astype(f32), pad], axis=0
    ).T
    cols_ref[...] = cols
    earlier = (iota((tok, tok), 1) < iota((tok, tok), 0)).astype(f32)
    owner = iota((tok, 128), 1)
    low = (owner * shard).astype(f32)
    lane = iota((tok, code_ref.shape[2]), 1)
    codes = [[0.0, 0.0] for _ in range(groups)]
    for f in range(feats):
        ids = cols[:, f : f + 1]
        mine = ((ids >= low) & (ids < low + shard) & (owner < groups)).astype(f32)
        rank = mm(earlier, mine)
        slot = jnp.sum(mine * (rank + (owner * cap).astype(f32)), axis=1, keepdims=True)
        slot = slot.astype(jnp.int32)
        for k in range(groups):
            hit = (slot + (f - k) * cap == lane) & (mine[:, k : k + 1] > 0.0)
            local = ids - k * shard
            coarse = jnp.floor(local * (1.0 / high))
            for i, value in enumerate((coarse, local - coarse * high)):
                codes[k][i] = codes[k][i] + jnp.sum(jnp.where(hit, value, 0.0), axis=0, keepdims=True)
        pick_ref[f] = (slot == iota((tok, groups * cap), 1)).astype(f32).astype(bf16)
        quot = cols[:, feats + f : feats + f + 1].astype(jnp.int32)
        onehot = (quot == iota((tok, table_ref.shape[1]), 1)).astype(f32).astype(bf16)
        q_ref[:, f * width : (f + 1) * width] = mm(onehot, table_ref[f])
    which = iota(code_ref.shape[1:], 0)
    for k in range(groups):
        code_ref[k] = jnp.where(which == 0, codes[k][0], jnp.where(which == 1, codes[k][1], 0.0)).astype(bf16)


def step_body(
    core_ref, recv_ref, pick_ref, q_ref, cols_ref, code_ref, w1_ref, b1_ref, w2_ref, b2_ref,
    loss_ref, rem_ref, keep_ref, send_ref, tiny_ref,
    joined_s, qgrad_s, onehot_s, *, cap, parts,
):
    groups = recv_ref.shape[0]
    feats, tok, _ = pick_ref.shape
    width = recv_ref.shape[2]
    hid = w1_ref.shape[1]
    rows = onehot_s.shape[2]
    core = core_ref[0]
    preact = jnp.broadcast_to(b1_ref[...], (tok, hid))
    total = jnp.zeros((tok, hid), f32)
    rem_parts = []
    for f in range(feats):
        got = recv_ref[:, f * cap : (f + 1) * cap, :].reshape(groups * cap, width)
        rem = mm(pick_ref[f], got)
        rem_parts.append(rem)
        joined = (q_ref[:, f * width : (f + 1) * width] * rem).astype(bf16)
        joined_s[f] = joined
        total = total + mm(joined, w1_ref[f * width : (f + 1) * width, :])
        quot = cols_ref[:, feats + f : feats + f + 1].astype(jnp.int32)
        onehot_s[f] = (quot == iota((tok, rows), 1)).astype(f32)
    preact = total + preact
    sig = jax.nn.sigmoid(preact)
    hidden = (preact * sig).astype(bf16).astype(f32)
    w2_row = w2_ref[...].astype(f32)
    logits = jnp.sum(hidden * w2_row, axis=1, keepdims=True) + b2_ref[0]
    target = cols_ref[:, 2 * feats : 2 * feats + 1]
    loss = jnp.maximum(logits, 0.0) + jnp.log1p(jnp.exp(-jnp.abs(logits))) - target * logits
    loss_ref[...] = jnp.broadcast_to(loss, (tok, tok)).T[0:1, :]
    dlogits = jax.nn.sigmoid(logits) - target
    slopes = sig * (1.0 + preact * (1.0 - sig))
    dpre = dlogits * w2_row * slopes
    tiny_ref[0:1, :] = jnp.sum(dpre, axis=0, keepdims=True)
    tiny_ref[1:2, :] = jnp.sum(dlogits * hidden, axis=0, keepdims=True)
    tiny_ref[2:3, :] = jnp.sum(jnp.broadcast_to(dlogits, (tok, hid)), axis=0, keepdims=True)
    tiny_ref[3:TINY, :] = jnp.zeros((TINY - 3, hid), f32)
    rounded = dpre.astype(bf16)
    piece = width // parts
    packed = []
    for f in range(feats):
        djoined = mm(rounded, w1_ref[f * width : (f + 1) * width, :], ((1,), (1,)))
        qgrad_s[f] = djoined * rem_parts[f]
        rem_grad = (djoined * q_ref[:, f * width : (f + 1) * width]).astype(bf16)
        packed.append(mm(pick_ref[f], rem_grad, ((0,), (0,))))
    for d in range(parts):
        both = [p[:, d * piece : (d + 1) * piece] for p in packed]
        both = jnp.concatenate(both, axis=1).astype(bf16)
        rem_ref[d, :, 0:cap, :] = both.reshape(groups, cap, feats * piece)
        rem_ref[d, :, cap:, :] = code_ref[...]
    for which, out_ref in ((1 - core, send_ref), (core, keep_ref)):
        grad_w = mm(joined_s[which], rounded, ((0,), (0,)))
        grad_q = mm(onehot_s[which], qgrad_s[which], ((0,), (0,)), precision=lax.Precision.HIGHEST)
        out_ref[0:width, :] = grad_w.astype(out_ref.dtype)
        out_ref[width : width + rows, :] = grad_q.astype(out_ref.dtype)
    send_ref[width + rows :, :] = pack_tiny(tiny_ref[0:1, :], tiny_ref[1:2, :], tiny_ref[2:3, :])


def pair_body(me_ref, keep_ref, tiny_ref, recv_ref, *refs):
    out_refs, all_s = refs[:-1], refs[-1]
    parts, rows = all_s.shape[0], all_s.shape[1] - TINY
    me = me_ref[0]
    got = unpack_tiny(recv_ref[parts * rows :, :])
    tiny = pack_tiny(*(tiny_ref[i : i + 1, :] + got[i] for i in range(3)))
    for p in range(parts):
        at = slice(p * rows, (p + 1) * rows)
        all_s[p, 0:rows, :] = (keep_ref[at, :] + recv_ref[at, :].astype(f32)).astype(bf16)
        all_s[p, rows:, :] = tiny
    for k in range(parts):
        out_refs[k][...] = all_s[me ^ k]


def plane_body(*refs):
    recv_refs, out_ref = refs[:-1], refs[-1]
    rows = out_ref.shape[0] - TINY
    out_ref[0:rows, :] = tree_sum(r[0:rows, :].astype(f32) for r in recv_refs).astype(bf16)
    tiny = [unpack_tiny(r[rows:, :]) for r in recv_refs]
    out_ref[rows:, :] = pack_tiny(*(tree_sum(t[i] for t in tiny) for i in range(3)))


def add_body(mine_ref, recv_ref, out_ref):
    rows = mine_ref.shape[0] - TINY
    out_ref[0:rows, :] = (mine_ref[0:rows, :].astype(f32) + recv_ref[0:rows, :].astype(f32)).astype(bf16)
    mine, got = unpack_tiny(mine_ref[rows:, :]), unpack_tiny(recv_ref[rows:, :])
    out_ref[rows:, :] = pack_tiny(*(a + b for a, b in zip(mine, got)))


def last_body(mine_ref, recv_ref, out_ref, b1_ref, w2_ref, b2_ref):
    rows = mine_ref.shape[0] - TINY
    out_ref[...] = (mine_ref[0:rows, :].astype(f32) + recv_ref[0:rows, :].astype(f32)).astype(bf16)
    mine, got = unpack_tiny(mine_ref[rows:, :]), unpack_tiny(recv_ref[rows:, :])
    b1_ref[...] = mine[0] + got[0]
    w2_ref[...] = mine[1] + got[1]
    b2_ref[...] = (mine[2] + got[2])[:, 0:1]


def final_body(core_ref, mine_ref, other_ref, w1_ref, quot_ref):
    core = core_ref[0]
    width = w1_ref.shape[1]
    for which, ref in ((core, mine_ref), (1 - core, other_ref)):
        w1_ref[which] = ref[0:width, :].astype(f32)
        quot_ref[which] = ref[width:, :].astype(f32)


def scatter_body(grads_ref, out_ref, e_s, *, high, cap):
    feats, piece, shard = out_ref.shape
    steps = shard // high
    chunk = e_s.shape[1]
    total = grads_ref.shape[0]
    some = chunk // cap
    accs = [jnp.zeros((steps * piece, high), f32) for _ in range(feats)]
    for at in range(0, total, some):
        values = grads_ref[at : at + some, 0:cap, :].astype(f32).reshape(chunk, feats * piece).T
        codes = [grads_ref[at + i, cap:, :].astype(f32) for i in range(some)]
        for f in range(feats):
            code = jnp.concatenate([c[:, f * cap : (f + 1) * cap] for c in codes], axis=1).astype(jnp.int32)
            hot = (iota((high, chunk), 0) == code[1:2, :]).astype(f32).astype(bf16)
            mine = values[f * piece : (f + 1) * piece, :]
            for s in range(steps):
                e_s[s * piece : (s + 1) * piece, :] = jnp.where(code[0:1, :] == s, mine, 0.0).astype(bf16)
            accs[f] = accs[f] + mm(e_s[...], hot, ((1,), (1,)))
    for f in range(feats):
        for s in range(steps):
            out_ref[f, :, s * high : (s + 1) * high] = accs[f][s * piece : (s + 1) * piece, :]


def on_device(quot_ids, rem_ids, labels, quot_table, rem_table, w1, b1, w2, b2, *, sizes):
    nz, ny, nx, nc = sizes
    dp, grp = nz * ny, nx * nc
    tok, feats = rem_ids.shape
    shard, width = rem_table.shape[1], rem_table.shape[2]
    rows_q = quot_table.shape[1]
    hid = w1.shape[1]
    cap = 2 * tok // grp
    piece = width // dp
    struct = jax.ShapeDtypeStruct
    core = lax.axis_index("c")[None]
    me = (lax.axis_index("x") * nc + lax.axis_index("c"))[None]

    ids_all = lax.all_gather(rem_ids.T.reshape(-1), ("x", "c"), tiled=True).reshape(grp * feats, tok)
    picked = call(
        functools.partial(fetch_body, cap=cap), struct((grp, feats * cap, width), bf16),
        (me, ids_all, rem_table), [SM, VM, VM],
    )
    recv = lax.all_to_all(picked, ("x", "c"), 0, 0, tiled=True)

    pick, q_rows, cols, codes = call(
        functools.partial(slots_body, shard=shard, cap=cap, groups=grp, high=HIGH),
        (
            struct((feats, tok, grp * cap), bf16), struct((tok, feats * width), f32), struct((tok, 8), f32),
            struct((grp, TINY, feats * piece), bf16),
        ),
        (rem_ids.T, quot_ids.T, labels[None, :], quot_table),
        [VM] * 4,
    )
    half = width + rows_q
    loss, rem_send, keep, send, tiny = call(
        functools.partial(step_body, cap=cap, parts=dp),
        (
            struct((1, tok), f32),
            struct((dp, grp, cap + TINY, feats * piece), bf16),
            struct((half, hid), f32),
            struct((half + TINY, hid), bf16),
            struct((TINY, hid), f32),
        ),
        (core, recv, pick, q_rows, cols, codes, w1, b1[None, :], w2[None, :], b2),
        [SM] + [VM] * 8 + [SM],
        [
            pltpu.VMEM((feats, tok, width), bf16),
            pltpu.VMEM((feats, tok, width), f32),
            pltpu.VMEM((feats, tok, rows_q), f32),
        ],
    )
    swap = [(i, i ^ 1) for i in range(nc)]
    other = lax.ppermute(send, "c", swap)
    rem_send = rem_send.reshape(dp * grp, cap + TINY, feats * piece)
    rem_got = lax.all_to_all(rem_send, ("z", "y", "x", "c"), 0, 0, tiled=True)

    plane = ny * nx
    part = half // plane
    spot = (lax.axis_index("y") * nx + lax.axis_index("x"))[None]
    wire = struct((part + TINY, hid), bf16)
    blocks = call(
        pair_body, (wire,) * plane, (spot, keep, tiny, other), [SM] + [VM] * 3,
        [pltpu.VMEM((plane, part + TINY, hid), bf16)],
    )
    got = [
        lax.ppermute(blocks[k], ("y", "x"), [(i, i ^ k) for i in range(plane)]) for k in range(1, plane)
    ]
    block = call(plane_body, wire, (blocks[0], *got), [VM] * plane)
    step = 1
    while step < nz:
        got = lax.ppermute(block, "z", [(i, i ^ step) for i in range(nz)])
        step *= 2
        if step < nz:
            block = call(add_body, wire, (block, got), [VM] * 2)
        else:
            row = struct((1, hid), f32)
            block, sum_b1, sum_w2, sum_b2 = call(
                last_body, (struct((part, hid), bf16), row, row, struct((1, 1), f32)), (block, got), [VM] * 2
            )

    grad_rem = call(
        functools.partial(scatter_body, high=HIGH, cap=cap),
        struct((feats, piece, shard), f32),
        (rem_got,),
        [VM],
        [pltpu.VMEM((shard // HIGH * piece, 512), bf16)],
    )
    block = lax.all_gather(block, ("y", "x"), tiled=True)
    other = lax.ppermute(block, "c", swap)
    grad_w1, grad_quot = call(
        final_body,
        (struct((feats, width, hid), f32), struct((feats, rows_q, width), f32)),
        (core, block, other),
        [SM, VM, VM],
    )
    return (
        loss.reshape(tok), grad_rem.transpose(0, 2, 1), grad_quot, grad_w1.reshape(feats * width, hid),
        sum_b1.reshape(hid), sum_w2.reshape(hid), sum_b2.reshape(1),
    )


def solution(mesh):
    dp, grp = mesh.shape["dp"], mesh.shape["grp"]
    sizes = (dp // 2, 2, grp // 2, 2)
    fine = Mesh(mesh.devices.reshape(sizes), ("z", "y", "x", "c"))
    every, group, data = ("z", "y", "x", "c"), ("x", "c"), ("z", "y")
    placed = (P(every, None), P(every, None), P(every), P(), P(None, group, None), P(), P(), P(), P())
    return jax.shard_map(
        functools.partial(on_device, sizes=sizes),
        mesh=fine,
        in_specs=placed,
        out_specs=(P(every), P(None, group, data), P(), P(), P(), P(), P()),
        check_vma=False,
    )
```

time: 263 us -> 100 us (0.38)
  blocking collectives: 79.2 us -> 19.2 us
  other arithmetic: 55.4 us -> 0 us
  waiting for transfers between devices: 62.9 us -> 26.1 us
  Pallas kernels: 0 us -> 30.7 us
  local copies, waits for them, and re-layouts: 33.9 us -> 6.01 us
  between operations: 14.7 us -> 1.39 us
  starting transfers between devices: 5.49 us -> 16.6 us
  matrix products: 10.9 us -> 0 us
    unnamed x5 -> x0, other arithmetic: 50 us -> none
    psum x1 -> x0, blocking collectives: 40.5 us -> none  [on_device(): lax.psum((grad_w1, grad_b1, grad_w2, grad_b2, grad_quot), ('dp', 'grp'))]
    psum x1 -> x0, waiting for transfers between devices: 37.7 us -> none  [on_device(): lax.psum((grad_w1, grad_b1, grad_w2, grad_b2, grad_quot), ('dp', 'grp'))]
    pallas_call x0 -> x9, Pallas kernels: none -> 30.7 us  [call(): pl.pallas_call(body, out_shape=outs, in_specs=in_specs, out_specs=tuple((...]
    reduce_scatter x1 -> x0, waiting for transfers between devices: 25.1 us -> none  [on_device(): lax.psum_scatter(partial_value.astype(jnp.bfloat16), 'grp', scatter_dimen...]
    ppermute x0 -> x7, waiting for transfers between devices: none -> 21.3 us  [the longest x2 16.2 us: on_device(): got = lax.ppermute(block, 'z', [(i, i ^ step) for i in range(nz)])]
    all_gather x2, blocking collectives: 38.7 us -> 19.2 us  [the longest x1 11.3 us: on_device(): block = lax.all_gather(block, ('y', 'x'), tiled=True)]
    dot_general x9 -> x0, matrix products: 10.9 us -> none  [the longest x1 2.82 us: on_device(): grad_w1 = jnp.dot(joined.T, rounded, preferred_element_type=jnp.float32)]
  transfers between devices with their start and end apart: 4 -> 9, of which waited for: 2 -> 5; matrix products, arithmetic and copies ran while one was open for 26% -> 1% of each run, Pallas kernels for 0% -> 13%
where the time goes in v1:
time: 100 us; the launch traced here: 99.9 us
  Pallas kernels  30.7 us (31%)
  waiting for transfers between devices  26.1 us (26%)
  blocking collectives  19.2 us (19%)
  starting transfers between devices  16.6 us (17%)
  local copies, waits for them, and re-layouts  6.01 us (6%)
  between operations  1.39 us (1%)
    pallas_call x9, Pallas kernels, call(): pl.pallas_call(body, out_shape=outs, in_specs=in_specs, out_specs=tuple((...  30.7 us
    ppermute x2, waiting for transfers between devices, on_device(): got = lax.ppermute(block, 'z', [(i, i ^ step) for i in range(nz)])  16.2 us
    all_gather x1, blocking collectives, on_device(): block = lax.all_gather(block, ('y', 'x'), tiled=True)  11.3 us
    all_gather x1, blocking collectives, on_device(): lax.all_gather(rem_ids.T.reshape(-1), ('x', 'c'), tiled=True)  7.93 us
    unnamed x22, local copies, waits for them, and re-layouts  5.43 us
    all_to_all x1, starting transfers between devices, on_device(): rem_got = lax.all_to_all(rem_send, ('z', 'y', 'x', 'c'), 0, 0, tiled=True)  4.92 us
    all_to_all x1, waiting for transfers between devices, on_device(): recv = lax.all_to_all(picked, ('x', 'c'), 0, 0, tiled=True)  4.75 us
    ppermute x2, starting transfers between devices, on_device(): got = lax.ppermute(block, 'z', [(i, i ^ step) for i in range(nz)])  4.6 us
  transfers between devices with their start and end apart: 9, of which 5 were waited for; matrix products, arithmetic and copies ran while one was open for 1% of the time, Pallas kernels for 13%

profile of v1, /device:TPU:0, one launch (start us, length us, event | category | flops | bytes accessed | tf_op | source)
XLA Modules:
  0.0 99.9 jit_solution(2907177632021102839)
XLA Ops:
  0.6 7.9 %all-gather = s32[4,1,256]{2,1,0:T(1,128)} all-gather(s32[1,1,256]{2,1,0:T(1,128)} %bitcast.20), channel_id=1, replica_groups=mesh['z'=4,'y'=2,'x'=2,'c'=2] {'x','c'}, dimensions={0}, use_global_device_ids=true | all-gather | bytes 5120 | tf_op jit(solution)/shard_map/all_gather | solution.py:275
  8.6 0.0 copy-start.10
  8.6 6.8 %shard_map.144 = bf16[4,128,512]{2,1,0:T(8,128)(2,1)} custom-call(s32[1]{0:T(128)} %bitcast.1.me_ref, s32[8,128]{1,0:T(8,128)} %bitcast.19, bf16[2,4096,512]{2,1,0:T(8,128)(2,1)} %table_ref.2), custom_call_target="tpu_custom_call" | custom-call | tf_op jit(solution)/shard_map/pallas_call | solution.py:29
  15.4 3.5 %all-to-all-start = ((bf16[4,128,512]{2,1,0:T(8,128)(2,1)}), bf16[4,128,512]{2,1,0:T(8,128)(2,1)S(1)}, u32[]{:S(2)}, u32[]{:S(2)}) async-start(bf16[4,128,512]{2,1,0:T(8,128)(2,1)} %shard_map.144), calls=%async_computation | async-start | bytes 1048576 | tf_op jit(solution)/shard_map/all_to_all | solution.py:280
  19.5 0.0 copy-done.10
  19.6 0.6 broadcast_in_dim.22.w2_ref
  20.1 2.8 %shard_map.145 = (bf16[2,128,256]{2,1,0:T(8,128)(2,1)}, f32[128,1024]{1,0:T(8,128)}, f32[128,8]{1,0:T(8,128)}, bf16[4,8,128]{2,1,0:T(8,128)(2,1)}) custom-call(s32[2,128]{1,0:T(2,128)} %bitcast.21, s32[2,128]{1,0:T(2,128)} %bitcast.23, s32[1,128]{1,0:T(1,128)} %bitcast.24, bf16[2,128,512]{2,1,0:T(8,128)(2,1)} %table_ref.3), custom_call_target="tpu_custom_call" | custom-call | tf_op jit(solution)/shard_map/pallas_call | solution.py:29
  22.9 4.7 %all-to-all-done.recv_ref = bf16[4,128,512]{2,1,0:T(8,128)(2,1)S(1)} async-done(((bf16[4,128,512]{2,1,0:T(8,128)(2,1)}), bf16[4,128,512]{2,1,0:T(8,128)(2,1)S(1)}, u32[]{:S(2)}, u32[]{:S(2)}) %all-to-all-start) | async-done | bytes 524320 | tf_op jit(solution)/shard_map/all_to_all | solution.py:280
  27.7 0.0 copy-start.2
  27.7 0.8 copy-done.2
  28.5 5.0 %shard_map.146 = (f32[1,128]{1,0:T(1,128)}, bf16[8,4,72,128]{3,2,1,0:T(8,128)(2,1)}, f32[640,512]{1,0:T(8,128)}, bf16[648,512]{1,0:T(8,128)(2,1)}, f32[8,512]{1,0:T(8,128)}) custom-call(s32[1]{0:T(128)} %bitcast.core_ref, bf16[4,128,512]{2,1,0:T(8,128)(2,1)} %copy-done.2, bf16[2,128,256]{2,1,0:T(8,128)(2,1)} %get-tuple-element.26.pick_ref, ...), custom_call_target="tpu_custom_call" | custom-call | tf_op jit(solution)/shard_map/pallas_call | solution.py:29
  33.5 0.0 collective-permute-start
  33.5 2.3 %collective-permute-done.recv_ref = bf16[648,512]{1,0:T(8,128)(2,1)S(1)} collective-permute-done((bf16[648,512]{1,0:T(8,128)(2,1)}, bf16[648,512]{1,0:T(8,128)(2,1)S(1)}, u32[]{:S(2)}, u32[]{:S(2)}) %collective-permute-start) | collective-permute-done | bytes 663584 | tf_op jit(solution)/shard_map/ppermute | solution.py:310
  35.8 0.0 copy-start.3
  35.8 0.8 copy-done.3
  36.6 2.6 %shard_map.148 = (bf16[168,512]{1,0:T(8,128)(2,1)}, bf16[168,512]{1,0:T(8,128)(2,1)}, bf16[168,512]{1,0:T(8,128)(2,1)}, bf16[168,512]{1,0:T(8,128)(2,1)}) custom-call(s32[1]{0:T(128)} %bitcast.11.me_ref, f32[640,512]{1,0:T(8,128)} %get-tuple-element.32.keep_ref, f32[8,512]{1,0:T(8,128)} %get-tuple-element.33.tiny_ref, bf16[648,512]{1,0:T(8,128)(2,1)} %copy-done.3), custom_call_target="tpu_custom_call" | custom-call | tf_op jit(solution)/shard_map/pallas_call | solution.py:29
  39.2 0.4 collective-permute-start.1
  39.6 1.5 %collective-permute-start.2 = (bf16[168,512]{1,0:T(8,128)(2,1)}, bf16[168,512]{1,0:T(8,128)(2,1)S(1)}, u32[]{:S(2)}, u32[]{:S(2)}) collective-permute-start(bf16[168,512]{1,0:T(8,128)(2,1)} %get-tuple-element.37), channel_id=1, source_target_pairs={{0,4},{2,6},{4,0},{6,2},{1,5},{3,7},{5,1},{7,3},{8,12},{10,14},{12... | collective-permute-start | bytes 516104 | tf_op jit(solution)/shard_map/ppermute | solution.py:323
  41.2 1.6 %collective-permute-start.3 = (bf16[168,512]{1,0:T(8,128)(2,1)}, bf16[168,512]{1,0:T(8,128)(2,1)S(1)}, u32[]{:S(2)}, u32[]{:S(2)}) collective-permute-start(bf16[168,512]{1,0:T(8,128)(2,1)} %get-tuple-element.38), channel_id=1, source_target_pairs={{0,6},{2,4},{4,2},{6,0},{1,7},{3,5},{5,3},{7,1},{8,14},{10,12},{12... | collective-permute-start | bytes 516104 | tf_op jit(solution)/shard_map/ppermute | solution.py:323
  42.7 4.9 %all-to-all-start.1 = ((bf16[32,72,128]{2,1,0:T(8,128)(2,1)}), bf16[32,72,128]{2,1,0:T(8,128)(2,1)S(1)}, u32[]{:S(2)}, u32[]{:S(2)}) async-start(bf16[32,72,128]{2,1,0:T(8,128)(2,1)} %bitcast.18), calls=%async_computation.1 | async-start | bytes 1179648 | tf_op jit(solution)/shard_map/all_to_all | solution.py:312
  47.7 0.0 collective-permute-done.1.refs_1_
  47.7 0.0 copy-start.5
  47.7 0.0 collective-permute-done.2.refs_2_
  47.7 0.0 copy-start.6
  47.7 2.8 %collective-permute-done.3.refs_3_ = bf16[168,512]{1,0:T(8,128)(2,1)S(1)} collective-permute-done((bf16[168,512]{1,0:T(8,128)(2,1)}, bf16[168,512]{1,0:T(8,128)(2,1)S(1)}, u32[]{:S(2)}, u32[]{:S(2)}) %collective-permute-start.3) | collective-permute-done | bytes 172064 | tf_op jit(solution)/shard_map/ppermute | solution.py:323
  50.5 0.0 copy-start.7
  50.5 0.0 copy-done.5
  50.5 0.0 copy-done.6
  50.5 0.7 copy-done.7
  51.2 2.1 %shard_map.149.mine_ref = bf16[168,512]{1,0:T(8,128)(2,1)} custom-call(bf16[168,512]{1,0:T(8,128)(2,1)} %get-tuple-element.35.refs_0_, bf16[168,512]{1,0:T(8,128)(2,1)} %copy-done.5, bf16[168,512]{1,0:T(8,128)(2,1)} %copy-done.6, bf16[168,512]{1,0:T(8,128)(2,1)} %copy-done.7), custom_call_target="tpu_custom_call" | custom-call | tf_op jit(solution)/shard_map/pallas_call | solution.py:29
  53.3 1.6 %collective-permute-start.4 = (bf16[168,512]{1,0:T(8,128)(2,1)}, bf16[168,512]{1,0:T(8,128)(2,1)S(1)}, u32[]{:S(2)}, u32[]{:S(2)}) collective-permute-start(bf16[168,512]{1,0:T(8,128)(2,1)} %shard_map.149.mine_ref), channel_id=1, source_target_pairs={{0,8},{8,0},{16,24},{24,16},{1,9},{9,1},{17,25},{25,17},{2,10},{10... | collective-permute-start | bytes 516104 | tf_op jit(solution)/shard_map/ppermute | solution.py:328
  54.8 8.2 %collective-permute-done.4.recv_ref = bf16[168,512]{1,0:T(8,128)(2,1)S(1)} collective-permute-done((bf16[168,512]{1,0:T(8,128)(2,1)}, bf16[168,512]{1,0:T(8,128)(2,1)S(1)}, u32[]{:S(2)}, u32[]{:S(2)}) %collective-permute-start.4) | collective-permute-done | bytes 172064 | tf_op jit(solution)/shard_map/ppermute | solution.py:328
  63.1 0.0 copy-start.9
  63.1 0.7 copy-done.9
  63.7 1.8 %shard_map.150.mine_ref = bf16[168,512]{1,0:T(8,128)(2,1)} custom-call(bf16[168,512]{1,0:T(8,128)(2,1)} %shard_map.149.mine_ref, bf16[168,512]{1,0:T(8,128)(2,1)} %copy-done.9), custom_call_target="tpu_custom_call" | custom-call | tf_op jit(solution)/shard_map/pallas_call | solution.py:29
  65.6 3.0 %collective-permute-start.5 = (bf16[168,512]{1,0:T(8,128)(2,1)}, bf16[168,512]{1,0:T(8,128)(2,1)S(1)}, u32[]{:S(2)}, u32[]{:S(2)}) collective-permute-start(bf16[168,512]{1,0:T(8,128)(2,1)} %shard_map.150.mine_ref), channel_id=1, source_target_pairs={{0,16},{8,24},{16,0},{24,8},{1,17},{9,25},{17,1},{25,9},{2,18},{10... | collective-permute-start | bytes 516104 | tf_op jit(solution)/shard_map/ppermute | solution.py:328
  68.6 8.0 %collective-permute-done.5.recv_ref = bf16[168,512]{1,0:T(8,128)(2,1)S(1)} collective-permute-done((bf16[168,512]{1,0:T(8,128)(2,1)}, bf16[168,512]{1,0:T(8,128)(2,1)S(1)}, u32[]{:S(2)}, u32[]{:S(2)}) %collective-permute-start.5) | collective-permute-done | bytes 172064 | tf_op jit(solution)/shard_map/ppermute | solution.py:328
  76.6 0.0 copy-start.8
  76.6 0.7 copy-done.8
  77.2 1.8 %shard_map.151 = (bf16[160,512]{1,0:T(8,128)(2,1)}, f32[1,512]{1,0:T(1,128)}, f32[1,512]{1,0:T(1,128)}, f32[1,1]{1,0:T(1,128)}) custom-call(bf16[168,512]{1,0:T(8,128)(2,1)} %shard_map.150.mine_ref, bf16[168,512]{1,0:T(8,128)(2,1)} %copy-done.8), custom_call_target="tpu_custom_call" | custom-call | tf_op jit(solution)/shard_map/pallas_call | solution.py:29
  79.0 11.3 %all_gather.7.mine_ref = bf16[640,512]{1,0:T(8,128)(2,1)S(1)} all-gather(bf16[160,512]{1,0:T(8,128)(2,1)} %get-tuple-element.39), channel_id=1, replica_groups=mesh['z'=4,'y'=2,'x'=2,'c'=2] {'y','x'}, dimensions={0}, use_global_device_ids=true | all-gather | bytes 819200 | tf_op jit(solution)/shard_map/all_gather | solution.py:345
  90.3 0.0 copy-start
  90.3 0.1 collective-permute-start.6
  90.4 0.0 all-to-all-done.1.grads_ref
  90.4 0.0 copy-start.1
  90.4 0.9 copy-done.1
  91.3 4.8 %shard_map.147 = f32[2,64,4096]{2,1,0:T(8,128)} custom-call(bf16[32,72,128]{2,1,0:T(8,128)(2,1)} %copy-done.1), custom_call_target="tpu_custom_call" | custom-call | tf_op jit(solution)/shard_map/pallas_call | solution.py:29
  96.1 0.0 collective-permute-done.6.other_ref
  96.1 0.0 copy-done
  96.1 0.0 copy-start.4
  96.1 0.9 copy-done.4
  97.0 2.9 %shard_map.152 = (f32[2,512,512]{2,1,0:T(8,128)}, f32[2,128,512]{2,1,0:T(8,128)}) custom-call(s32[1]{0:T(128)} %bitcast.core_ref, bf16[640,512]{1,0:T(8,128)(2,1)} %copy-done, bf16[640,512]{1,0:T(8,128)(2,1)} %copy-done.4), custom_call_target="tpu_custom_call" | custom-call | tf_op jit(solution)/shard_map/pallas_call | solution.py:29
Async XLA Ops:
  8.6 11.0 %copy-start.10 = (bf16[512]{0:T(512)(128)(2,1)S(1)}, bf16[512]{0:T(512)(128)(2,1)}, u32[]{:S(2)}) copy-start(bf16[512]{0:T(512)(128)(2,1)} %param.16) | copy-start | bytes 3076
  15.4 12.3 %all-to-all-start = ((bf16[4,128,512]{2,1,0:T(8,128)(2,1)}), bf16[4,128,512]{2,1,0:T(8,128)(2,1)S(1)}, u32[]{:S(2)}, u32[]{:S(2)}) async-start(bf16[4,128,512]{2,1,0:T(8,128)(2,1)} %shard_map.144), calls=%async_computation | async-start | bytes 1048576 | tf_op jit(solution)/shard_map/all_to_all | solution.py:280
  27.7 0.8 copy-start.2
  33.5 2.3 %collective-permute-start = (bf16[648,512]{1,0:T(8,128)(2,1)}, bf16[648,512]{1,0:T(8,128)(2,1)S(1)}, u32[]{:S(2)}, u32[]{:S(2)}) collective-permute-start(bf16[648,512]{1,0:T(8,128)(2,1)} %get-tuple-element.34), channel_id=1, source_target_pairs={{0,1},{1,0},{2,3},{3,2},{4,5},{5,4},{6,7},{7,6},{8,9},{9,8},{10,11... | collective-permute-start | bytes 1990664 | tf_op jit(solution)/shard_map/ppermute | solution.py:310
  35.8 0.8 copy-start.3
  39.2 8.4 %collective-permute-start.1 = (bf16[168,512]{1,0:T(8,128)(2,1)}, bf16[168,512]{1,0:T(8,128)(2,1)S(1)}, u32[]{:S(2)}, u32[]{:S(2)}) collective-permute-start(bf16[168,512]{1,0:T(8,128)(2,1)} %get-tuple-element.36), channel_id=1, source_target_pairs={{0,2},{2,0},{4,6},{6,4},{1,3},{3,1},{5,7},{7,5},{8,10},{10,8},{12,... | collective-permute-start | bytes 516104 | tf_op jit(solution)/shard_map/ppermute | solution.py:323
  39.6 8.1 %collective-permute-start.2 = (bf16[168,512]{1,0:T(8,128)(2,1)}, bf16[168,512]{1,0:T(8,128)(2,1)S(1)}, u32[]{:S(2)}, u32[]{:S(2)}) collective-permute-start(bf16[168,512]{1,0:T(8,128)(2,1)} %get-tuple-element.37), channel_id=1, source_target_pairs={{0,4},{2,6},{4,0},{6,2},{1,5},{3,7},{5,1},{7,3},{8,12},{10,14},{12... | collective-permute-start | bytes 516104 | tf_op jit(solution)/shard_map/ppermute | solution.py:323
  41.2 9.4 %collective-permute-start.3 = (bf16[168,512]{1,0:T(8,128)(2,1)}, bf16[168,512]{1,0:T(8,128)(2,1)S(1)}, u32[]{:S(2)}, u32[]{:S(2)}) collective-permute-start(bf16[168,512]{1,0:T(8,128)(2,1)} %get-tuple-element.38), channel_id=1, source_target_pairs={{0,6},{2,4},{4,2},{6,0},{1,7},{3,5},{5,3},{7,1},{8,14},{10,12},{12... | collective-permute-start | bytes 516104 | tf_op jit(solution)/shard_map/ppermute | solution.py:323
  42.7 47.6 %all-to-all-start.1 = ((bf16[32,72,128]{2,1,0:T(8,128)(2,1)}), bf16[32,72,128]{2,1,0:T(8,128)(2,1)S(1)}, u32[]{:S(2)}, u32[]{:S(2)}) async-start(bf16[32,72,128]{2,1,0:T(8,128)(2,1)} %bitcast.18), calls=%async_computation.1 | async-start | bytes 1179648 | tf_op jit(solution)/shard_map/all_to_all | solution.py:312
  47.7 2.8 %copy-start.5 = (bf16[168,512]{1,0:T(8,128)(2,1)}, bf16[168,512]{1,0:T(8,128)(2,1)S(1)}, u32[]{:S(2)}) copy-start(bf16[168,512]{1,0:T(8,128)(2,1)S(1)} %collective-permute-done.1.refs_1_) | copy-start | bytes 516100
  47.7 2.8 %copy-start.6 = (bf16[168,512]{1,0:T(8,128)(2,1)}, bf16[168,512]{1,0:T(8,128)(2,1)S(1)}, u32[]{:S(2)}) copy-start(bf16[168,512]{1,0:T(8,128)(2,1)S(1)} %collective-permute-done.2.refs_2_) | copy-start | bytes 516100
  50.5 0.7 copy-start.7
  53.3 9.8 %collective-permute-start.4 = (bf16[168,512]{1,0:T(8,128)(2,1)}, bf16[168,512]{1,0:T(8,128)(2,1)S(1)}, u32[]{:S(2)}, u32[]{:S(2)}) collective-permute-start(bf16[168,512]{1,0:T(8,128)(2,1)} %shard_map.149.mine_ref), channel_id=1, source_target_pairs={{0,8},{8,0},{16,24},{24,16},{1,9},{9,1},{17,25},{25,17},{2,10},{10... | collective-permute-start | bytes 516104 | tf_op jit(solution)/shard_map/ppermute | solution.py:328
  63.1 0.7 copy-start.9
  65.6 11.0 %collective-permute-start.5 = (bf16[168,512]{1,0:T(8,128)(2,1)}, bf16[168,512]{1,0:T(8,128)(2,1)S(1)}, u32[]{:S(2)}, u32[]{:S(2)}) collective-permute-start(bf16[168,512]{1,0:T(8,128)(2,1)} %shard_map.150.mine_ref), channel_id=1, source_target_pairs={{0,16},{8,24},{16,0},{24,8},{1,17},{9,25},{17,1},{25,9},{2,18},{10... | collective-permute-start | bytes 516104 | tf_op jit(solution)/shard_map/ppermute | solution.py:328
  76.6 0.7 copy-start.8
  90.3 5.8 %copy-start = (bf16[640,512]{1,0:T(8,128)(2,1)}, bf16[640,512]{1,0:T(8,128)(2,1)S(1)}, u32[]{:S(2)}) copy-start(bf16[640,512]{1,0:T(8,128)(2,1)S(1)} %all_gather.7.mine_ref) | copy-start | bytes 1966084
  90.3 5.8 %collective-permute-start.6 = (bf16[640,512]{1,0:T(8,128)(2,1)S(1)}, bf16[640,512]{1,0:T(8,128)(2,1)S(1)}, u32[]{:S(2)}, u32[]{:S(2)}) collective-permute-start(bf16[640,512]{1,0:T(8,128)(2,1)S(1)} %all_gather.7.mine_ref), channel_id=1, source_target_pairs={{0,1},{1,0},{2,3},{3,2},{4,5},{5,4},{6,7},{7,6},{8,9},{9,8},{10,11... | collective-permute-start | bytes 1966088 | tf_op jit(solution)/shard_map/ppermute | solution.py:346
  90.4 0.9 copy-start.1
  96.1 0.9 copy-start.4

commit v2 on v1

--- a/solution.py
+++ b/solution.py
@@ -76,29 +76,48 @@
     return b1_row, w2_row, jnp.broadcast_to(b2_row, b1_row.shape)
 
 
-def fetch_body(me_ref, ids_ref, table_ref, out_ref, *, cap):
+def fetch_body(me_ref, ids_ref, table_ref, *refs, cap):
+    out_refs, (key_s, value_s, table_s, sems) = refs[:-4], refs[-4:]
     n_rows, tok = ids_ref.shape
-    feats, shard, _ = table_ref.shape
+    feats, shard, width = table_ref.shape
+    chunks, chunk = table_s.shape[1], table_s.shape[2]
     groups = n_rows // feats
-    local = ids_ref[...] - me_ref[0] * shard
+    copies = [
+        [
+            pltpu.make_async_copy(
+                table_ref.at[f, pl.ds(c * chunk, chunk), :], table_s.at[f, c], sems.at[f, c]
+            )
+            for c in range(chunks)
+        ]
+        for f in range(feats)
+    ]
+    for row in copies:
+        for copy in row:
+            copy.start()
+    me = me_ref[0]
+    local = ids_ref[...] - me * shard
     mine = (local >= 0) & (local < shard)
     before = (iota((tok, tok), 0) < iota((tok, tok), 1)).astype(f32)
-    key = jnp.where(mine, mm(mine.astype(f32), before), -1.0).astype(jnp.int32)
-    value = local.astype(f32)
+    key_s[...] = jnp.where(mine, mm(mine.astype(f32), before), -1.0).astype(jnp.int32)
+    value_s[...] = local.astype(f32)
     slot = iota((cap, tok), 0)
     for f in range(feats):
         cols = []
         for k in range(groups):
-            at = slice(k * feats + f, k * feats + f + 1)
-            hit = jnp.where(key[at, :] == slot, value[at, :], 0.0)
+            at = (me ^ k) * feats + f
+            hit = jnp.where(key_s[pl.ds(at, 1), :] == slot, value_s[pl.ds(at, 1), :], 0.0)
             cols.append(jnp.sum(hit, axis=1, keepdims=True))
         col = jnp.concatenate(cols, axis=0).astype(jnp.int32)
-        hot = (col == iota((groups * cap, shard), 1)).astype(f32).astype(bf16)
-        got = mm(hot, table_ref[f]).astype(bf16)
-        out_ref[:, f * cap : (f + 1) * cap, :] = got.reshape(groups, cap, got.shape[1])
-
-
-def slots_body(rem_ref, quot_ref, label_ref, table_ref, pick_ref, q_ref, cols_ref, code_ref, *, shard, cap, groups, high):
+        got = jnp.zeros((groups * cap, width), f32)
+        for c in range(chunks):
+            hot = (col - c * chunk == iota((groups * cap, chunk), 1)).astype(f32).astype(bf16)
+            copies[f][c].wait()
+            got = got + mm(hot, table_s[f, c])
+        for k in range(groups):
+            out_refs[k][f * cap : (f + 1) * cap, :] = got[k * cap : (k + 1) * cap].astype(bf16)
+
+
+def slots_body(me_ref, rem_ref, quot_ref, label_ref, table_ref, pick_ref, q_ref, cols_ref, code_ref, *, shard, cap, groups, high):
     feats, tok = rem_ref.shape
     width = table_ref.shape[2]
     pad = jnp.zeros((8 - 2 * feats - 1, tok), f32)
@@ -108,7 +127,9 @@
     cols_ref[...] = cols
     earlier = (iota((tok, tok), 1) < iota((tok, tok), 0)).astype(f32)
     owner = iota((tok, 128), 1)
-    low = (owner * shard).astype(f32)
+    me = me_ref[0]
+    turn = iota((tok, 128), 1) ^ me
+    low = (turn * shard).astype(f32)
     lane = iota((tok, code_ref.shape[2]), 1)
     codes = [[0.0, 0.0] for _ in range(groups)]
     for f in range(feats):
@@ -119,7 +140,7 @@
         slot = slot.astype(jnp.int32)
         for k in range(groups):
             hit = (slot + (f - k) * cap == lane) & (mine[:, k : k + 1] > 0.0)
-            local = ids - k * shard
+            local = ids - ((me ^ k) * shard).astype(f32)
             coarse = jnp.floor(local * (1.0 / high))
             for i, value in enumerate((coarse, local - coarse * high)):
                 codes[k][i] = codes[k][i] + jnp.sum(jnp.where(hit, value, 0.0), axis=0, keepdims=True)
@@ -132,22 +153,35 @@
         code_ref[k] = jnp.where(which == 0, codes[k][0], jnp.where(which == 1, codes[k][1], 0.0)).astype(bf16)
 
 
-def step_body(
-    core_ref, recv_ref, pick_ref, q_ref, cols_ref, code_ref, w1_ref, b1_ref, w2_ref, b2_ref,
-    loss_ref, rem_ref, keep_ref, send_ref, tiny_ref,
-    joined_s, qgrad_s, onehot_s, *, cap, parts,
-):
-    groups = recv_ref.shape[0]
+def store_parts(out_ref, start, value):
+    part = out_ref.part
+    at = 0
+    while at < value.shape[0]:
+        p, inner = divmod(start + at, part)
+        many = min(part - inner, value.shape[0] - at)
+        out_ref.ref[p, inner : inner + many, :] = value[at : at + many].astype(out_ref.ref.dtype)
+        at += many
+
+
+class Parts:
+    def __init__(self, ref, part):
+        self.ref, self.part = ref, part
+
+
+def step_body(spot_ref, pick_ref, q_ref, cols_ref, code_ref, w1_ref, b1_ref, w2_ref, b2_ref, *refs, cap, parts, part):
+    loss_ref, rem_ref, keep_ref, send_ref, joined_s, qgrad_s, onehot_s, tiny_ref = refs[-8:]
+    recv_refs = refs[:-8]
     feats, tok, _ = pick_ref.shape
-    width = recv_ref.shape[2]
+    groups = len(recv_refs)
+    width = recv_refs[0].shape[1]
     hid = w1_ref.shape[1]
     rows = onehot_s.shape[2]
-    core = core_ref[0]
+    core, me = spot_ref[0], spot_ref[1]
     preact = jnp.broadcast_to(b1_ref[...], (tok, hid))
     total = jnp.zeros((tok, hid), f32)
     rem_parts = []
     for f in range(feats):
-        got = recv_ref[:, f * cap : (f + 1) * cap, :].reshape(groups * cap, width)
+        got = jnp.concatenate([r[f * cap : (f + 1) * cap, :] for r in recv_refs], axis=0)
         rem = mm(pick_ref[f], got)
         rem_parts.append(rem)
         joined = (q_ref[:, f * width : (f + 1) * width] * rem).astype(bf16)
@@ -181,60 +215,35 @@
     for d in range(parts):
         both = [p[:, d * piece : (d + 1) * piece] for p in packed]
         both = jnp.concatenate(both, axis=1).astype(bf16)
-        rem_ref[d, :, 0:cap, :] = both.reshape(groups, cap, feats * piece)
-        rem_ref[d, :, cap:, :] = code_ref[...]
+        for k in range(groups):
+            rem_ref[d, me ^ k, 0:cap, :] = both[k * cap : (k + 1) * cap]
+            rem_ref[d, me ^ k, cap:, :] = code_ref[k]
     for which, out_ref in ((1 - core, send_ref), (core, keep_ref)):
         grad_w = mm(joined_s[which], rounded, ((0,), (0,)))
         grad_q = mm(onehot_s[which], qgrad_s[which], ((0,), (0,)), precision=lax.Precision.HIGHEST)
-        out_ref[0:width, :] = grad_w.astype(out_ref.dtype)
-        out_ref[width : width + rows, :] = grad_q.astype(out_ref.dtype)
-    send_ref[width + rows :, :] = pack_tiny(tiny_ref[0:1, :], tiny_ref[1:2, :], tiny_ref[2:3, :])
-
-
-def pair_body(me_ref, keep_ref, tiny_ref, recv_ref, *refs):
-    out_refs, all_s = refs[:-1], refs[-1]
-    parts, rows = all_s.shape[0], all_s.shape[1] - TINY
-    me = me_ref[0]
-    got = unpack_tiny(recv_ref[parts * rows :, :])
-    tiny = pack_tiny(*(tiny_ref[i : i + 1, :] + got[i] for i in range(3)))
-    for p in range(parts):
-        at = slice(p * rows, (p + 1) * rows)
-        all_s[p, 0:rows, :] = (keep_ref[at, :] + recv_ref[at, :].astype(f32)).astype(bf16)
-        all_s[p, rows:, :] = tiny
-    for k in range(parts):
-        out_refs[k][...] = all_s[me ^ k]
+        store_parts(Parts(out_ref, part), 0, grad_w)
+        store_parts(Parts(out_ref, part), width, grad_q)
+    tiny = pack_tiny(tiny_ref[0:1, :], tiny_ref[1:2, :], tiny_ref[2:3, :])
+    for p in range(send_ref.shape[0]):
+        send_ref[p, part:, :] = tiny
 
 
 def plane_body(*refs):
     recv_refs, out_ref = refs[:-1], refs[-1]
     rows = out_ref.shape[0] - TINY
     out_ref[0:rows, :] = tree_sum(r[0:rows, :].astype(f32) for r in recv_refs).astype(bf16)
-    tiny = [unpack_tiny(r[rows:, :]) for r in recv_refs]
+    tiny = []
+    for r in recv_refs:
+        mine, other = unpack_tiny(r[rows : rows + TINY, :]), unpack_tiny(r[rows + TINY :, :])
+        tiny.append([a + b for a, b in zip(mine, other)])
     out_ref[rows:, :] = pack_tiny(*(tree_sum(t[i] for t in tiny) for i in range(3)))
 
 
-def add_body(mine_ref, recv_ref, out_ref):
-    rows = mine_ref.shape[0] - TINY
-    out_ref[0:rows, :] = (mine_ref[0:rows, :].astype(f32) + recv_ref[0:rows, :].astype(f32)).astype(bf16)
-    mine, got = unpack_tiny(mine_ref[rows:, :]), unpack_tiny(recv_ref[rows:, :])
-    out_ref[rows:, :] = pack_tiny(*(a + b for a, b in zip(mine, got)))
-
-
-def last_body(mine_ref, recv_ref, out_ref, b1_ref, w2_ref, b2_ref):
-    rows = mine_ref.shape[0] - TINY
-    out_ref[...] = (mine_ref[0:rows, :].astype(f32) + recv_ref[0:rows, :].astype(f32)).astype(bf16)
-    mine, got = unpack_tiny(mine_ref[rows:, :]), unpack_tiny(recv_ref[rows:, :])
-    b1_ref[...] = mine[0] + got[0]
-    w2_ref[...] = mine[1] + got[1]
-    b2_ref[...] = (mine[2] + got[2])[:, 0:1]
-
-
-def final_body(core_ref, mine_ref, other_ref, w1_ref, quot_ref):
-    core = core_ref[0]
-    width = w1_ref.shape[1]
-    for which, ref in ((core, mine_ref), (1 - core, other_ref)):
-        w1_ref[which] = ref[0:width, :].astype(f32)
-        quot_ref[which] = ref[width:, :].astype(f32)
+def last_body(rows_ref, b1_ref, w2_ref, b2_ref):
+    tiny = [unpack_tiny(rows_ref[at : at + TINY, :]) for at in range(0, rows_ref.shape[0], TINY)]
+    b1_ref[...] = tree_sum(t[0] for t in tiny)
+    w2_ref[...] = tree_sum(t[1] for t in tiny)
+    b2_ref[...] = tree_sum(t[2] for t in tiny)[:, 0:1]
 
 
 def scatter_body(grads_ref, out_ref, e_s, *, high, cap):
@@ -274,36 +283,48 @@
 
     ids_all = lax.all_gather(rem_ids.T.reshape(-1), ("x", "c"), tiled=True).reshape(grp * feats, tok)
     picked = call(
-        functools.partial(fetch_body, cap=cap), struct((grp, feats * cap, width), bf16),
-        (me, ids_all, rem_table), [SM, VM, VM],
-    )
-    recv = lax.all_to_all(picked, ("x", "c"), 0, 0, tiled=True)
-
-    pick, q_rows, cols, codes = call(
+        functools.partial(fetch_body, cap=cap),
+        (struct((feats * cap, width), bf16),) * grp,
+        (me, ids_all, rem_table),
+        [SM, VM, pl.BlockSpec(memory_space=pl.ANY)],
+        [
+            pltpu.VMEM((grp * feats, tok), jnp.int32), pltpu.VMEM((grp * feats, tok), f32),
+            pltpu.VMEM((feats, 4, shard // 4, width), bf16), pltpu.SemaphoreType.DMA((feats, 4)),
+        ],
+    )
+    recv = [picked[0]] + [lax.ppermute(picked[k], ("x", "c"), [(i, i ^ k) for i in range(grp)]) for k in range(1, grp)]
+
+    slots = call(
         functools.partial(slots_body, shard=shard, cap=cap, groups=grp, high=HIGH),
         (
             struct((feats, tok, grp * cap), bf16), struct((tok, feats * width), f32), struct((tok, 8), f32),
             struct((grp, TINY, feats * piece), bf16),
         ),
-        (rem_ids.T, quot_ids.T, labels[None, :], quot_table),
-        [VM] * 4,
-    )
+        (me, rem_ids.T, quot_ids.T, labels[None, :], quot_table),
+        [SM] + [VM] * 4,
+    )
+    pick, q_rows, cols, codes = slots
+
     half = width + rows_q
-    loss, rem_send, keep, send, tiny = call(
-        functools.partial(step_body, cap=cap, parts=dp),
+    plane = ny * nx
+    part = half // plane
+    loss, rem_send, keep, send = call(
+        functools.partial(step_body, cap=cap, parts=dp, part=part),
         (
             struct((1, tok), f32),
             struct((dp, grp, cap + TINY, feats * piece), bf16),
-            struct((half, hid), f32),
-            struct((half + TINY, hid), bf16),
-            struct((TINY, hid), f32),
+            struct((plane, part, hid), f32),
+            struct((plane, part + TINY, hid), bf16),
         ),
-        (core, recv, pick, q_rows, cols, codes, w1, b1[None, :], w2[None, :], b2),
-        [SM] + [VM] * 8 + [SM],
+        (
+            jnp.concatenate([core, me]), pick, q_rows, cols, codes, w1, b1[None, :], w2[None, :], b2, *recv,
+        ),
+        [SM] + [VM] * 7 + [SM] + [VM] * len(recv),
         [
             pltpu.VMEM((feats, tok, width), bf16),
             pltpu.VMEM((feats, tok, width), f32),
             pltpu.VMEM((feats, tok, rows_q), f32),
+            pltpu.VMEM((TINY, hid), f32),
         ],
     )
     swap = [(i, i ^ 1) for i in range(nc)]
@@ -311,29 +332,31 @@
     rem_send = rem_send.reshape(dp * grp, cap + TINY, feats * piece)
     rem_got = lax.all_to_all(rem_send, ("z", "y", "x", "c"), 0, 0, tiled=True)
 
-    plane = ny * nx
-    part = half // plane
-    spot = (lax.axis_index("y") * nx + lax.axis_index("x"))[None]
+    spot = lax.axis_index("y") * nx + lax.axis_index("x")
     wire = struct((part + TINY, hid), bf16)
-    blocks = call(
-        pair_body, (wire,) * plane, (spot, keep, tiny, other), [SM] + [VM] * 3,
-        [pltpu.VMEM((plane, part + TINY, hid), bf16)],
-    )
+    blocks = []
+    for k in range(plane):
+        kept = lax.dynamic_index_in_dim(keep, spot ^ k, 0, keepdims=False)
+        came = lax.dynamic_index_in_dim(other, spot ^ k, 0, keepdims=False)
+        main = (kept + came[:part].astype(f32)).astype(bf16)
+        blocks.append(jnp.concatenate([main, send[0, part:], other[0, part:]]))
     got = [
         lax.ppermute(blocks[k], ("y", "x"), [(i, i ^ k) for i in range(plane)]) for k in range(1, plane)
     ]
     block = call(plane_body, wire, (blocks[0], *got), [VM] * plane)
+    main, tiny_rows = block[:part], block[part:]
     step = 1
     while step < nz:
         got = lax.ppermute(block, "z", [(i, i ^ step) for i in range(nz)])
         step *= 2
+        main = (main.astype(f32) + got[:part].astype(f32)).astype(bf16)
+        tiny_rows = jnp.concatenate([tiny_rows, got[part:]])
         if step < nz:
-            block = call(add_body, wire, (block, got), [VM] * 2)
-        else:
-            row = struct((1, hid), f32)
-            block, sum_b1, sum_w2, sum_b2 = call(
-                last_body, (struct((part, hid), bf16), row, row, struct((1, 1), f32)), (block, got), [VM] * 2
-            )
+            block = lax.optimization_barrier(jnp.concatenate([main, tiny_rows]))
+            main, tiny_rows = block[:part], block[part:]
+    main = lax.optimization_barrier(main)
+    row = struct((1, hid), f32)
+    sum_b1, sum_w2, sum_b2 = call(last_body, (row, row, struct((1, 1), f32)), (tiny_rows,), [VM])
 
     grad_rem = call(
         functools.partial(scatter_body, high=HIGH, cap=cap),
@@ -342,14 +365,11 @@
         [VM],
         [pltpu.VMEM((shard // HIGH * piece, 512), bf16)],
     )
-    block = lax.all_gather(block, ("y", "x"), tiled=True)
+    block = lax.all_gather(main, ("y", "x"), tiled=True)
     other = lax.ppermute(block, "c", swap)
-    grad_w1, grad_quot = call(
-        final_body,
-        (struct((feats, width, hid), f32), struct((feats, rows_q, width), f32)),
-        (core, block, other),
-        [SM, VM, VM],
-    )
+    first, second = jnp.where(core == 0, block, other), jnp.where(core == 0, other, block)
+    grad_w1 = jnp.stack([first[:width], second[:width]]).astype(f32)
+    grad_quot = jnp.stack([first[width:], second[width:]]).astype(f32)
     return (
         loss.reshape(tok), grad_rem.transpose(0, 2, 1), grad_quot, grad_w1.reshape(feats * width, hid),
         sum_b1.reshape(hid), sum_w2.reshape(hid), sum_b2.reshape(1),

time: 100 us -> 99.4 us (level)
  Pallas kernels: 30.7 us -> 22.4 us
  other arithmetic: 0 us -> 7.11 us
  waiting for transfers between devices: 26.1 us -> 30.9 us
  starting transfers between devices: 16.6 us -> 14.2 us
  local copies, waits for them, and re-layouts: 6.01 us -> 4.26 us
    pallas_call x9 -> x6, Pallas kernels: 30.7 us -> 22.4 us  [call(): pl.pallas_call(body, out_shape=outs, in_specs=in_specs, out_specs=tuple((...]
    ppermute x3, waiting for transfers between devices: 2.81 us -> 8.2 us  [on_device(): lax.ppermute(blocks[k], ('y', 'x'), [(i, i ^ k) for i in range(plane)])]
    convert_element_type x0 -> x5, other arithmetic: none -> 4.98 us  [the longest x1 1.68 us: on_device(): grad_w1 = jnp.stack([first[:width], second[:width]]).astype(f32)]
    all_to_all x1 -> x0, waiting for transfers between devices: 4.75 us -> none  [on_device(): recv = lax.all_to_all(picked, ('x', 'c'), 0, 0, tiled=True)]
    ppermute x2, waiting for transfers between devices: 16.2 us -> 19.7 us  [on_device(): got = lax.ppermute(block, 'z', [(i, i ^ step) for i in range(nz)])]
    all_to_all x1 -> x0, starting transfers between devices: 3.47 us -> none  [on_device(): recv = lax.all_to_all(picked, ('x', 'c'), 0, 0, tiled=True)]
    unnamed x22 -> x16, local copies, waits for them, and re-layouts: 5.43 us -> 2.19 us
    concatenate x0 -> x4, other arithmetic: none -> 1.94 us  [the longest x1 0.72 us: on_device(): blocks.append(jnp.concatenate([main, send[0, part:], other[0, part:]]))]
  transfers between devices with their start and end apart: 9 -> 11, of which waited for: 5 -> 7; matrix products, arithmetic and copies ran while one was open for 1% -> 4% of each run, Pallas kernels for 13% -> 9%
where the time goes in v2:
time: 99.4 us; the launch traced here: 98.8 us
  waiting for transfers between devices  30.9 us (31%)
  Pallas kernels  22.4 us (23%)
  blocking collectives  18.4 us (19%)
  starting transfers between devices  14.2 us (14%)
  other arithmetic  7.11 us (7%)
  local copies, waits for them, and re-layouts  4.26 us (4%)
  between operations  1.43 us (1%)
    pallas_call x6, Pallas kernels, call(): pl.pallas_call(body, out_shape=outs, in_specs=in_specs, out_specs=tuple((...  22.4 us
    ppermute x2, waiting for transfers between devices, on_device(): got = lax.ppermute(block, 'z', [(i, i ^ step) for i in range(nz)])  19.7 us
    all_gather x1, blocking collectives, on_device(): block = lax.all_gather(main, ('y', 'x'), tiled=True)  10.5 us
    ppermute x3, waiting for transfers between devices, on_device(): lax.ppermute(blocks[k], ('y', 'x'), [(i, i ^ k) for i in range(plane)])  8.2 us
    all_gather x1, blocking collectives, on_device(): lax.all_gather(rem_ids.T.reshape(-1), ('x', 'c'), tiled=True)  7.91 us
    ppermute x2, starting transfers between devices, on_device(): got = lax.ppermute(block, 'z', [(i, i ^ step) for i in range(nz)])  4.23 us
    all_to_all x1, starting transfers between devices, on_device(): rem_got = lax.all_to_all(rem_send, ('z', 'y', 'x', 'c'), 0, 0, tiled=True)  3.97 us
    ppermute x3, starting transfers between devices, on_device(): lax.ppermute(blocks[k], ('y', 'x'), [(i, i ^ k) for i in range(plane)])  3.49 us
  transfers between devices with their start and end apart: 11, of which 7 were waited for; matrix products, arithmetic and copies ran while one was open for 4% of the time, Pallas kernels for 9%

profile of v2, /device:TPU:0, one launch (start us, length us, event | category | flops | bytes accessed | tf_op | source)
XLA Modules:
  0.0 98.8 jit_solution(9369143167657672329)
XLA Ops:
  0.6 7.9 %all-gather = s32[4,1,256]{2,1,0:T(1,128)} all-gather(s32[1,1,256]{2,1,0:T(1,128)} %bitcast.41), channel_id=1, replica_groups=mesh['z'=4,'y'=2,'x'=2,'c'=2] {'x','c'}, dimensions={0}, use_global_device_ids=true | all-gather | bytes 5120 | tf_op jit(solution)/shard_map/all_gather | solution.py:284
  8.6 0.0 copy-start.7
  8.6 6.3 %shard_map.145 = (bf16[128,512]{1,0:T(8,128)(2,1)}, bf16[128,512]{1,0:T(8,128)(2,1)}, bf16[128,512]{1,0:T(8,128)(2,1)}, bf16[128,512]{1,0:T(8,128)(2,1)}) custom-call(s32[1]{0:T(128)} %bitcast.1.me_ref, s32[8,128]{1,0:T(8,128)} %bitcast.40, bf16[2,4096,512]{2,1,0:T(8,128)(2,1)} %table_ref.3), custom_call_target="tpu_custom_call" | custom-call | tf_op jit(solution)/shard_map/pallas_call | solution.py:29
  14.9 0.4 collective-permute-start
  15.3 0.8 collective-permute-start.1
  16.0 0.7 collective-permute-start.2
  17.4 0.0 copy-done.7
  17.4 0.6 broadcast_in_dim.30.w2_ref
  18.0 2.8 %shard_map.144 = (bf16[2,128,256]{2,1,0:T(8,128)(2,1)}, f32[128,1024]{1,0:T(8,128)}, f32[128,8]{1,0:T(8,128)}, bf16[4,8,128]{2,1,0:T(8,128)(2,1)}) custom-call(s32[1]{0:T(128)} %bitcast.1.me_ref, s32[2,128]{1,0:T(2,128)} %bitcast.42, s32[2,128]{1,0:T(2,128)} %bitcast.44, s32[1,128]{1,0:T(1,128)} %bitcast.45, bf16[2,128,512]{2,1,0:T(8,128)(2,1)} %table_ref.2), custom_call_target="tpu_custom_call" | custom-call | tf_op jit(solution)/shard_map/pallas_call | solution.py:29
  20.8 0.6 pad_add_fusion.spot_ref
  21.4 0.0 collective-permute-done.refs_1_
  21.4 0.0 copy-start.4
  21.4 0.5 collective-permute-done.1.refs_2_
  21.8 0.0 copy-start.5
  21.8 1.2 %collective-permute-done.2.refs_3_ = bf16[128,512]{1,0:T(8,128)(2,1)S(1)} collective-permute-done((bf16[128,512]{1,0:T(8,128)(2,1)}, bf16[128,512]{1,0:T(8,128)(2,1)S(1)}, u32[]{:S(2)}, u32[]{:S(2)}) %collective-permute-start.2) | collective-permute-done | bytes 131104 | tf_op jit(solution)/shard_map/ppermute | solution.py:295
  23.0 0.0 copy-start.6
  23.0 0.0 copy-done.4
  23.1 0.0 copy-done.5
  23.1 0.6 copy-done.6
  23.7 4.9 %shard_map.146 = (f32[1,128]{1,0:T(1,128)}, bf16[8,4,72,128]{3,2,1,0:T(8,128)(2,1)}, f32[4,160,512]{2,1,0:T(8,128)}, bf16[4,168,512]{2,1,0:T(8,128)(2,1)}) custom-call(s32[2]{0:T(128)} %pad_add_fusion.spot_ref, bf16[2,128,256]{2,1,0:T(8,128)(2,1)} %get-tuple-element.22.pick_ref, f32[128,1024]{1,0:T(8,128)} %get-tuple-element.23.q_ref, ...), custom_call_target="tpu_custom_call" | custom-call | tf_op jit(solution)/shard_map/pallas_call | solution.py:29
  28.6 0.6 collective-permute-start.3
  29.3 0.7 slice_bitcast_fusion.5
  30.0 1.3 %collective-permute-done.3 = bf16[4,168,512]{2,1,0:T(8,128)(2,1)S(1)} collective-permute-done((bf16[4,168,512]{2,1,0:T(8,128)(2,1)}, bf16[4,168,512]{2,1,0:T(8,128)(2,1)S(1)}, u32[]{:S(2)}, u32[]{:S(2)}) %collective-permute-start.3) | collective-permute-done | bytes 688160 | tf_op jit(solution)/shard_map/ppermute | solution.py:331
  31.2 1.5 %fusion.3 = (bf16[160,512]{1,0:T(8,128)(2,1)S(1)}, bf16[160,512]{1,0:T(8,128)(2,1)S(1)}, bf16[160,512]{1,0:T(8,128)(2,1)S(1)}, bf16[160,512]{1,0:T(8,128)(2,1)S(1)}) fusion(f32[4,160,512]{2,1,0:T(8,128)} %get-tuple-element.32, s32[]{:T(128)S(6)} %select_n.28, bf16[4,168,512]{2,1,0:T(8,128)(2,1)S(1)} %collective-permute-done.3, s32[]{:T(128)S(6)} %select_n.27, ...), kind=kLoop, calls=%fused_computation.25 | loop fusion | flops 983040 | bytes 2621456 | tf_op jit(solution)/shard_map/convert_element_type | solution.py:341
  32.7 0.7 pad_maximum_fusion.1
  33.5 1.7 %collective-permute-start.6 = (bf16[176,512]{1,0:T(8,128)(2,1)S(1)}, bf16[176,512]{1,0:T(8,128)(2,1)S(1)}, u32[]{:S(2)}, u32[]{:S(2)}) collective-permute-start(bf16[176,512]{1,0:T(8,128)(2,1)S(1)} %get-tuple-element.43), channel_id=1, source_target_pairs={{0,6},{2,4},{4,2},{6,0},{1,7},{3,5},{5,3},{7,1},{8,14},{10,12},{12... | collective-permute-start | bytes 540680 | tf_op jit(solution)/shard_map/ppermute | solution.py:344
  35.2 1.2 %collective-permute-start.4 = (bf16[176,512]{1,0:T(8,128)(2,1)S(1)}, bf16[176,512]{1,0:T(8,128)(2,1)S(1)}, u32[]{:S(2)}, u32[]{:S(2)}) collective-permute-start(bf16[176,512]{1,0:T(8,128)(2,1)S(1)} %get-tuple-element.44), channel_id=1, source_target_pairs={{0,2},{2,0},{4,6},{6,4},{1,3},{3,1},{5,7},{7,5},{8,10},{10,8},{12,... | collective-permute-start | bytes 540680 | tf_op jit(solution)/shard_map/ppermute | solution.py:344
  36.4 0.5 collective-permute-start.5
  36.9 4.9 %collective-permute-done.6.refs_3_ = bf16[176,512]{1,0:T(8,128)(2,1)S(1)} collective-permute-done((bf16[176,512]{1,0:T(8,128)(2,1)S(1)}, bf16[176,512]{1,0:T(8,128)(2,1)S(1)}, u32[]{:S(2)}, u32[]{:S(2)}) %collective-permute-start.6) | collective-permute-done | bytes 180256 | tf_op jit(solution)/shard_map/ppermute | solution.py:344
  41.8 0.0 copy-start.1
  41.8 3.3 %collective-permute-done.4.refs_1_ = bf16[176,512]{1,0:T(8,128)(2,1)S(1)} collective-permute-done((bf16[176,512]{1,0:T(8,128)(2,1)S(1)}, bf16[176,512]{1,0:T(8,128)(2,1)S(1)}, u32[]{:S(2)}, u32[]{:S(2)}) %collective-permute-start.4) | collective-permute-done | bytes 180256 | tf_op jit(solution)/shard_map/ppermute | solution.py:344
  45.1 0.0 copy-start.2
  45.1 0.0 collective-permute-done.5.refs_2_
  45.1 0.0 copy-start.3
  45.2 0.0 copy-done.1
  45.2 0.7 copy-done.2
  45.8 0.1 copy-done.3
  45.9 2.1 %shard_map.148 = bf16[168,512]{1,0:T(8,128)(2,1)} custom-call(bf16[176,512]{1,0:T(8,128)(2,1)} %get-tuple-element.46.refs_0_, bf16[176,512]{1,0:T(8,128)(2,1)} %copy-done.2, bf16[176,512]{1,0:T(8,128)(2,1)} %copy-done.3, bf16[176,512]{1,0:T(8,128)(2,1)} %copy-done.1), custom_call_target="tpu_custom_call" | custom-call | tf_op jit(solution)/shard_map/pallas_call | solution.py:29
  48.0 1.6 %collective-permute-start.7 = (bf16[168,512]{1,0:T(8,128)(2,1)}, bf16[168,512]{1,0:T(8,128)(2,1)S(1)}, u32[]{:S(2)}, u32[]{:S(2)}) collective-permute-start(bf16[168,512]{1,0:T(8,128)(2,1)} %shard_map.148), channel_id=1, source_target_pairs={{0,8},{8,0},{16,24},{24,16},{1,9},{9,1},{17,25},{25,17},{2,10},{10... | collective-permute-start | bytes 516104 | tf_op jit(solution)/shard_map/ppermute | solution.py:350
  49.6 4.0 %all-to-all-start = ((bf16[32,72,128]{2,1,0:T(8,128)(2,1)}), bf16[32,72,128]{2,1,0:T(8,128)(2,1)S(1)}, u32[]{:S(2)}, u32[]{:S(2)}) async-start(bf16[32,72,128]{2,1,0:T(8,128)(2,1)} %bitcast.9), calls=%async_computation | async-start | bytes 1179648 | tf_op jit(solution)/shard_map/all_to_all | solution.py:333
  53.5 0.7 slice.85
  54.2 0.1 collective-permute-done.7
  54.3 1.0 add_convert_fusion.1
  55.3 2.7 %collective-permute-start.8 = (bf16[176,512]{1,0:T(8,128)(2,1)S(1)}, bf16[176,512]{1,0:T(8,128)(2,1)S(1)}, u32[]{:S(2)}, u32[]{:S(2)}) collective-permute-start(bf16[176,512]{1,0:T(8,128)(2,1)S(1)} %pad_maximum_fusion.9), channel_id=1, source_target_pairs={{0,16},{8,24},{16,0},{24,8},{1,17},{9,25},{17,1},{25,9},{2,18},{10... | collective-permute-start | bytes 540680 | tf_op jit(solution)/shard_map/ppermute | solution.py:350
  58.0 19.7 %collective-permute-done.8 = bf16[176,512]{1,0:T(8,128)(2,1)S(1)} collective-permute-done((bf16[176,512]{1,0:T(8,128)(2,1)S(1)}, bf16[176,512]{1,0:T(8,128)(2,1)S(1)}, u32[]{:S(2)}, u32[]{:S(2)}) %collective-permute-start.8) | collective-permute-done | bytes 180256 | tf_op jit(solution)/shard_map/ppermute | solution.py:350
  77.7 10.5 %all_gather.7 = bf16[640,512]{1,0:T(8,128)(2,1)S(1)} all-gather(bf16[160,512]{1,0:T(8,128)(2,1)S(1)} %add_convert_fusion), channel_id=1, replica_groups=mesh['z'=4,'y'=2,'x'=2,'c'=2] {'y','x'}, dimensions={0}, use_global_device_ids=true | all-gather | bytes 819200 | tf_op jit(solution)/shard_map/all_gather | solution.py:368
  88.2 0.0 collective-permute-start.9
  88.2 0.0 all-to-all-done.grads_ref
  88.3 0.0 copy-start
  88.3 0.8 copy-done
  89.1 4.8 %shard_map.147 = f32[2,64,4096]{2,1,0:T(8,128)} custom-call(bf16[32,72,128]{2,1,0:T(8,128)(2,1)} %copy-done), custom_call_target="tpu_custom_call" | custom-call | tf_op jit(solution)/shard_map/pallas_call | solution.py:29
  93.9 0.6 pad_maximum_fusion.10.rows_ref
  94.5 1.4 %shard_map.149 = (f32[1,512]{1,0:T(1,128)}, f32[1,512]{1,0:T(1,128)}, f32[1,1]{1,0:T(1,128)}) custom-call(bf16[32,512]{1,0:T(8,128)(2,1)} %pad_maximum_fusion.10.rows_ref), custom_call_target="tpu_custom_call" | custom-call | tf_op jit(solution)/shard_map/pallas_call | solution.py:29
  95.9 0.0 collective-permute-done.9
  95.9 0.1 broadcast_select_fusion.1
  96.1 0.1 slice_bitcast_fusion
  96.1 0.1 pad_maximum_fusion
  96.2 1.7 %bitcast_convert_fusion = f32[1024,512]{1,0:T(8,128)} fusion(bf16[2,512,512]{2,1,0:T(8,128)(2,1)S(1)} %pad_maximum_fusion), kind=kLoop, calls=%fused_computation.1 | loop fusion | flops 524288 | bytes 3145728 | tf_op jit(solution)/shard_map/convert_element_type | solution.py:371
  97.9 0.8 maximum_convert_fusion
  (7 shorter events, 0.1 us)
Async XLA Ops:
  8.6 8.9 %copy-start.7 = (bf16[512]{0:T(512)(128)(2,1)S(1)}, bf16[512]{0:T(512)(128)(2,1)}, u32[]{:S(2)}) copy-start(bf16[512]{0:T(512)(128)(2,1)} %param.16) | copy-start | bytes 3076
  14.9 6.5 %collective-permute-start = (bf16[128,512]{1,0:T(8,128)(2,1)}, bf16[128,512]{1,0:T(8,128)(2,1)S(1)}, u32[]{:S(2)}, u32[]{:S(2)}) collective-permute-start(bf16[128,512]{1,0:T(8,128)(2,1)} %get-tuple-element.27), channel_id=1, source_target_pairs={{0,1},{1,0},{2,3},{3,2},{4,5},{5,4},{6,7},{7,6},{8,9},{9,8},{10,11... | collective-permute-start | bytes 393224 | tf_op jit(solution)/shard_map/ppermute | solution.py:295
  15.3 6.6 %collective-permute-start.1 = (bf16[128,512]{1,0:T(8,128)(2,1)}, bf16[128,512]{1,0:T(8,128)(2,1)S(1)}, u32[]{:S(2)}, u32[]{:S(2)}) collective-permute-start(bf16[128,512]{1,0:T(8,128)(2,1)} %get-tuple-element.28), channel_id=1, source_target_pairs={{0,2},{1,3},{2,0},{3,1},{4,6},{5,7},{6,4},{7,5},{8,10},{9,11},{10,... | collective-permute-start | bytes 393224 | tf_op jit(solution)/shard_map/ppermute | solution.py:295
  16.0 7.0 %collective-permute-start.2 = (bf16[128,512]{1,0:T(8,128)(2,1)}, bf16[128,512]{1,0:T(8,128)(2,1)S(1)}, u32[]{:S(2)}, u32[]{:S(2)}) collective-permute-start(bf16[128,512]{1,0:T(8,128)(2,1)} %get-tuple-element.29), channel_id=1, source_target_pairs={{0,3},{1,2},{2,1},{3,0},{4,7},{5,6},{6,5},{7,4},{8,11},{9,10},{10,... | collective-permute-start | bytes 393224 | tf_op jit(solution)/shard_map/ppermute | solution.py:295
  21.4 1.7 %copy-start.4 = (bf16[128,512]{1,0:T(8,128)(2,1)}, bf16[128,512]{1,0:T(8,128)(2,1)S(1)}, u32[]{:S(2)}) copy-start(bf16[128,512]{1,0:T(8,128)(2,1)S(1)} %collective-permute-done.refs_1_) | copy-start | bytes 393220
  21.8 1.2 %copy-start.5 = (bf16[128,512]{1,0:T(8,128)(2,1)}, bf16[128,512]{1,0:T(8,128)(2,1)S(1)}, u32[]{:S(2)}) copy-start(bf16[128,512]{1,0:T(8,128)(2,1)S(1)} %collective-permute-done.1.refs_2_) | copy-start | bytes 393220
  23.0 0.6 copy-start.6
  28.6 2.6 %collective-permute-start.3 = (bf16[4,168,512]{2,1,0:T(8,128)(2,1)}, bf16[4,168,512]{2,1,0:T(8,128)(2,1)S(1)}, u32[]{:S(2)}, u32[]{:S(2)}) collective-permute-start(bf16[4,168,512]{2,1,0:T(8,128)(2,1)} %get-tuple-element.33), channel_id=1, source_target_pairs={{0,1},{1,0},{2,3},{3,2},{4,5},{5,4},{6,7},{7,6},{8,9},{9,8},{10,11... | collective-permute-start | bytes 2064392 | tf_op jit(solution)/shard_map/ppermute | solution.py:331
  33.5 8.3 %collective-permute-start.6 = (bf16[176,512]{1,0:T(8,128)(2,1)S(1)}, bf16[176,512]{1,0:T(8,128)(2,1)S(1)}, u32[]{:S(2)}, u32[]{:S(2)}) collective-permute-start(bf16[176,512]{1,0:T(8,128)(2,1)S(1)} %get-tuple-element.43), channel_id=1, source_target_pairs={{0,6},{2,4},{4,2},{6,0},{1,7},{3,5},{5,3},{7,1},{8,14},{10,12},{12... | collective-permute-start | bytes 540680 | tf_op jit(solution)/shard_map/ppermute | solution.py:344
  35.2 10.0 %collective-permute-start.4 = (bf16[176,512]{1,0:T(8,128)(2,1)S(1)}, bf16[176,512]{1,0:T(8,128)(2,1)S(1)}, u32[]{:S(2)}, u32[]{:S(2)}) collective-permute-start(bf16[176,512]{1,0:T(8,128)(2,1)S(1)} %get-tuple-element.44), channel_id=1, source_target_pairs={{0,2},{2,0},{4,6},{6,4},{1,3},{3,1},{5,7},{7,5},{8,10},{10,8},{12,... | collective-permute-start | bytes 540680 | tf_op jit(solution)/shard_map/ppermute | solution.py:344
  36.4 8.7 %collective-permute-start.5 = (bf16[176,512]{1,0:T(8,128)(2,1)S(1)}, bf16[176,512]{1,0:T(8,128)(2,1)S(1)}, u32[]{:S(2)}, u32[]{:S(2)}) collective-permute-start(bf16[176,512]{1,0:T(8,128)(2,1)S(1)} %get-tuple-element.45), channel_id=1, source_target_pairs={{0,4},{2,6},{4,0},{6,2},{1,5},{3,7},{5,1},{7,3},{8,12},{10,14},{12... | collective-permute-start | bytes 540680 | tf_op jit(solution)/shard_map/ppermute | solution.py:344
  41.8 3.4 %copy-start.1 = (bf16[176,512]{1,0:T(8,128)(2,1)}, bf16[176,512]{1,0:T(8,128)(2,1)S(1)}, u32[]{:S(2)}) copy-start(bf16[176,512]{1,0:T(8,128)(2,1)S(1)} %collective-permute-done.6.refs_3_) | copy-start | bytes 540676
  45.1 0.7 copy-start.2
  45.1 0.7 copy-start.3
  48.0 6.3 %collective-permute-start.7 = (bf16[168,512]{1,0:T(8,128)(2,1)}, bf16[168,512]{1,0:T(8,128)(2,1)S(1)}, u32[]{:S(2)}, u32[]{:S(2)}) collective-permute-start(bf16[168,512]{1,0:T(8,128)(2,1)} %shard_map.148), channel_id=1, source_target_pairs={{0,8},{8,0},{16,24},{24,16},{1,9},{9,1},{17,25},{25,17},{2,10},{10... | collective-permute-start | bytes 516104 | tf_op jit(solution)/shard_map/ppermute | solution.py:350
  49.6 38.7 %all-to-all-start = ((bf16[32,72,128]{2,1,0:T(8,128)(2,1)}), bf16[32,72,128]{2,1,0:T(8,128)(2,1)S(1)}, u32[]{:S(2)}, u32[]{:S(2)}) async-start(bf16[32,72,128]{2,1,0:T(8,128)(2,1)} %bitcast.9), calls=%async_computation | async-start | bytes 1179648 | tf_op jit(solution)/shard_map/all_to_all | solution.py:333
  55.3 22.3 %collective-permute-start.8 = (bf16[176,512]{1,0:T(8,128)(2,1)S(1)}, bf16[176,512]{1,0:T(8,128)(2,1)S(1)}, u32[]{:S(2)}, u32[]{:S(2)}) collective-permute-start(bf16[176,512]{1,0:T(8,128)(2,1)S(1)} %pad_maximum_fusion.9), channel_id=1, source_target_pairs={{0,16},{8,24},{16,0},{24,8},{1,17},{9,25},{17,1},{25,9},{2,18},{10... | collective-permute-start | bytes 540680 | tf_op jit(solution)/shard_map/ppermute | solution.py:350
  88.2 7.7 %collective-permute-start.9 = (bf16[640,512]{1,0:T(8,128)(2,1)S(1)}, bf16[640,512]{1,0:T(8,128)(2,1)S(1)}, u32[]{:S(2)}, u32[]{:S(2)}) collective-permute-start(bf16[640,512]{1,0:T(8,128)(2,1)S(1)} %all_gather.7), channel_id=1, source_target_pairs={{0,1},{1,0},{2,3},{3,2},{4,5},{5,4},{6,7},{7,6},{8,9},{9,8},{10,11... | collective-permute-start | bytes 1966088 | tf_op jit(solution)/shard_map/ppermute | solution.py:369
  88.3 0.8 copy-start

commit v3 on v2

--- a/solution.py
+++ b/solution.py
@@ -66,14 +66,6 @@
         rest = rest - head
     out = jnp.where(which == 6, last, out)
     return out.astype(bf16)
-
-
-def unpack_tiny(block):
-    block = block.astype(f32)
-    b1_row = block[0:1] + block[1:2] + block[2:3]
-    w2_row = block[3:4] + block[4:5] + block[5:6]
-    b2_row = block[6:7, 0:1] + block[6:7, 1:2] + block[6:7, 2:3]
-    return b1_row, w2_row, jnp.broadcast_to(b2_row, b1_row.shape)
 
 
 def fetch_body(me_ref, ids_ref, table_ref, *refs, cap):
@@ -224,26 +216,10 @@
         store_parts(Parts(out_ref, part), 0, grad_w)
         store_parts(Parts(out_ref, part), width, grad_q)
     tiny = pack_tiny(tiny_ref[0:1, :], tiny_ref[1:2, :], tiny_ref[2:3, :])
+    empty = jnp.zeros(tiny.shape, f32)
     for p in range(send_ref.shape[0]):
-        send_ref[p, part:, :] = tiny
-
-
-def plane_body(*refs):
-    recv_refs, out_ref = refs[:-1], refs[-1]
-    rows = out_ref.shape[0] - TINY
-    out_ref[0:rows, :] = tree_sum(r[0:rows, :].astype(f32) for r in recv_refs).astype(bf16)
-    tiny = []
-    for r in recv_refs:
-        mine, other = unpack_tiny(r[rows : rows + TINY, :]), unpack_tiny(r[rows + TINY :, :])
-        tiny.append([a + b for a, b in zip(mine, other)])
-    out_ref[rows:, :] = pack_tiny(*(tree_sum(t[i] for t in tiny) for i in range(3)))
-
-
-def last_body(rows_ref, b1_ref, w2_ref, b2_ref):
-    tiny = [unpack_tiny(rows_ref[at : at + TINY, :]) for at in range(0, rows_ref.shape[0], TINY)]
-    b1_ref[...] = tree_sum(t[0] for t in tiny)
-    w2_ref[...] = tree_sum(t[1] for t in tiny)
-    b2_ref[...] = tree_sum(t[2] for t in tiny)[:, 0:1]
+        keep_ref[p, part:, :] = jnp.concatenate([tiny.astype(f32), empty], axis=0)
+        send_ref[p, part:, :] = jnp.concatenate([empty, tiny.astype(f32)], axis=0).astype(bf16)
 
 
 def scatter_body(grads_ref, out_ref, e_s, *, high, cap):
@@ -313,8 +289,8 @@
         (
             struct((1, tok), f32),
             struct((dp, grp, cap + TINY, feats * piece), bf16),
-            struct((plane, part, hid), f32),
-            struct((plane, part + TINY, hid), bf16),
+            struct((plane, part + 2 * TINY, hid), f32),
+            struct((plane, part + 2 * TINY, hid), bf16),
         ),
         (
             jnp.concatenate([core, me]), pick, q_rows, cols, codes, w1, b1[None, :], w2[None, :], b2, *recv,
@@ -333,30 +309,27 @@
     rem_got = lax.all_to_all(rem_send, ("z", "y", "x", "c"), 0, 0, tiled=True)
 
     spot = lax.axis_index("y") * nx + lax.axis_index("x")
-    wire = struct((part + TINY, hid), bf16)
     blocks = []
     for k in range(plane):
-        kept = lax.dynamic_index_in_dim(keep, spot ^ k, 0, keepdims=False)
-        came = lax.dynamic_index_in_dim(other, spot ^ k, 0, keepdims=False)
-        main = (kept + came[:part].astype(f32)).astype(bf16)
-        blocks.append(jnp.concatenate([main, send[0, part:], other[0, part:]]))
+        from_keep, from_other = lax.optimization_barrier((keep, other))
+        kept = lax.dynamic_index_in_dim(from_keep, spot ^ k, 0, keepdims=False)
+        came = lax.dynamic_index_in_dim(from_other, spot ^ k, 0, keepdims=False)
+        blocks.append((kept + came.astype(f32)).astype(bf16))
     got = [
         lax.ppermute(blocks[k], ("y", "x"), [(i, i ^ k) for i in range(plane)]) for k in range(1, plane)
     ]
-    block = call(plane_body, wire, (blocks[0], *got), [VM] * plane)
-    main, tiny_rows = block[:part], block[part:]
+    arrived = [blocks[0], *got]
+    main = tree_sum(r[:part].astype(f32) for r in arrived).astype(bf16)
+    main = lax.optimization_barrier(main)
+    tiny = tree_sum(r[part:].astype(f32) for r in arrived)
+    tiny = tiny[:TINY] + tiny[TINY:]
     step = 1
     while step < nz:
-        got = lax.ppermute(block, "z", [(i, i ^ step) for i in range(nz)])
+        swap_z = [(i, i ^ step) for i in range(nz)]
+        got = lax.ppermute(main, "z", swap_z)
+        tiny = tiny + lax.ppermute(tiny, "z", swap_z)
+        main = lax.optimization_barrier((main.astype(f32) + got.astype(f32)).astype(bf16))
         step *= 2
-        main = (main.astype(f32) + got[:part].astype(f32)).astype(bf16)
-        tiny_rows = jnp.concatenate([tiny_rows, got[part:]])
-        if step < nz:
-            block = lax.optimization_barrier(jnp.concatenate([main, tiny_rows]))
-            main, tiny_rows = block[:part], block[part:]
-    main = lax.optimization_barrier(main)
-    row = struct((1, hid), f32)
-    sum_b1, sum_w2, sum_b2 = call(last_body, (row, row, struct((1, 1), f32)), (tiny_rows,), [VM])
 
     grad_rem = call(
         functools.partial(scatter_body, high=HIGH, cap=cap),
@@ -372,7 +345,7 @@
     grad_quot = jnp.stack([first[width:], second[width:]]).astype(f32)
     return (
         loss.reshape(tok), grad_rem.transpose(0, 2, 1), grad_quot, grad_w1.reshape(feats * width, hid),
-        sum_b1.reshape(hid), sum_w2.reshape(hid), sum_b2.reshape(1),
+        tiny[0] + tiny[1] + tiny[2], tiny[3] + tiny[4] + tiny[5], jnp.sum(tiny[6, 0:3])[None],
     )
 
 

time: 99.4 us -> 103 us (1.036)
  waiting for transfers between devices: 30.9 us -> 40.9 us
  Pallas kernels: 22.4 us -> 18.9 us
  local copies, waits for them, and re-layouts: 4.26 us -> 2.14 us
    ppermute x2 -> x4, waiting for transfers between devices: 19.7 us -> 29 us  [the longest x2 20.7 us: on_device(): got = lax.ppermute(main, 'z', swap_z)]
    pallas_call x6 -> x4, Pallas kernels: 22.4 us -> 18.9 us  [call(): pl.pallas_call(body, out_shape=outs, in_specs=in_specs, out_specs=tuple((...]
    concatenate x3 -> x0, other arithmetic: 1.36 us -> none  [the longest x1 0.72 us: on_device(): blocks.append(jnp.concatenate([main, send[0, part:], other[0, part:]]))]
    convert_element_type x3 -> x4, other arithmetic: 2.47 us -> 1.7 us  [the longest x1 1.54 us: on_device(): blocks.append((kept + came.astype(f32)).astype(bf16))]
    unnamed x16 -> x10, local copies, waits for them, and re-layouts: 2.19 us -> 1.46 us
    ppermute x2 -> x4, starting transfers between devices: 4.23 us -> 4.37 us  [the longest x2 4.29 us: on_device(): got = lax.ppermute(main, 'z', swap_z)]
  transfers between devices with their start and end apart: 11 -> 13, of which waited for: 7 -> 10; matrix products, arithmetic and copies ran while one was open for 4% -> 2% of each run, Pallas kernels for 9% -> 7%
where the time goes in v3:
time: 103 us
  waiting for transfers between devices  40.9 us (40%)
  Pallas kernels  18.9 us (18%)
  blocking collectives  18.4 us (18%)
  starting transfers between devices  14.5 us (14%)
  other arithmetic  6.2 us (6%)
  local copies, waits for them, and re-layouts  2.14 us (2%)
  between operations  1.41 us (1%)
    ppermute x2, waiting for transfers between devices, on_device(): got = lax.ppermute(main, 'z', swap_z)  20.7 us
    pallas_call x4, Pallas kernels, call(): pl.pallas_call(body, out_shape=outs, in_specs=in_specs, out_specs=tuple((...  18.9 us
    all_gather x1, blocking collectives, on_device(): block = lax.all_gather(main, ('y', 'x'), tiled=True)  10.5 us
    ppermute x2, waiting for transfers between devices, on_device(): tiny = tiny + lax.ppermute(tiny, 'z', swap_z)  8.35 us
    ppermute x3, waiting for transfers between devices, on_device(): lax.ppermute(blocks[k], ('y', 'x'), [(i, i ^ k) for i in range(plane)])  8.2 us
    all_gather x1, blocking collectives, on_device(): lax.all_gather(rem_ids.T.reshape(-1), ('x', 'c'), tiled=True)  7.91 us
    ppermute x2, starting transfers between devices, on_device(): got = lax.ppermute(main, 'z', swap_z)  4.29 us
    all_to_all x1, starting transfers between devices, on_device(): rem_got = lax.all_to_all(rem_send, ('z', 'y', 'x', 'c'), 0, 0, tiled=True)  4.03 us
  transfers between devices with their start and end apart: 13, of which 10 were waited for; matrix products, arithmetic and copies ran while one was open for 2% of the time, Pallas kernels for 7%

profile of v3, /device:TPU:0, one launch (start us, length us, event | category | flops | bytes accessed | tf_op | source)
XLA Modules:
  0.0 102.5 jit_solution(5233123458492740545)
XLA Ops:
  0.6 7.9 %all-gather = s32[4,1,256]{2,1,0:T(1,128)} all-gather(s32[1,1,256]{2,1,0:T(1,128)} %bitcast.45), channel_id=1, replica_groups=mesh['z'=4,'y'=2,'x'=2,'c'=2] {'x','c'}, dimensions={0}, use_global_device_ids=true | all-gather | bytes 5120 | tf_op jit(solution)/shard_map/all_gather | solution.py:260
  8.6 0.0 copy-start.4
  8.6 6.3 %shard_map.145 = (bf16[128,512]{1,0:T(8,128)(2,1)}, bf16[128,512]{1,0:T(8,128)(2,1)}, bf16[128,512]{1,0:T(8,128)(2,1)}, bf16[128,512]{1,0:T(8,128)(2,1)}) custom-call(s32[1]{0:T(128)} %bitcast.1.me_ref, s32[8,128]{1,0:T(8,128)} %bitcast.44, bf16[2,4096,512]{2,1,0:T(8,128)(2,1)} %table_ref.3), custom_call_target="tpu_custom_call" | custom-call | tf_op jit(solution)/shard_map/pallas_call | solution.py:29
  14.8 0.4 collective-permute-start
  15.2 0.8 collective-permute-start.1
  16.0 0.7 collective-permute-start.2
  17.4 0.0 copy-done.4
  17.4 0.6 broadcast_in_dim.33.w2_ref
  18.0 2.8 %shard_map.144 = (bf16[2,128,256]{2,1,0:T(8,128)(2,1)}, f32[128,1024]{1,0:T(8,128)}, f32[128,8]{1,0:T(8,128)}, bf16[4,8,128]{2,1,0:T(8,128)(2,1)}) custom-call(s32[1]{0:T(128)} %bitcast.1.me_ref, s32[2,128]{1,0:T(2,128)} %bitcast.46, s32[2,128]{1,0:T(2,128)} %bitcast.50, s32[1,128]{1,0:T(1,128)} %bitcast.51, bf16[2,128,512]{2,1,0:T(8,128)(2,1)} %table_ref.2), custom_call_target="tpu_custom_call" | custom-call | tf_op jit(solution)/shard_map/pallas_call | solution.py:29
  20.8 0.6 pad_add_fusion.spot_ref
  21.4 0.0 collective-permute-done.refs_1_
  21.4 0.0 copy-start.1
  21.4 0.5 collective-permute-done.1.refs_2_
  21.8 0.0 copy-start.2
  21.8 1.2 %collective-permute-done.2.refs_3_ = bf16[128,512]{1,0:T(8,128)(2,1)S(1)} collective-permute-done((bf16[128,512]{1,0:T(8,128)(2,1)}, bf16[128,512]{1,0:T(8,128)(2,1)S(1)}, u32[]{:S(2)}, u32[]{:S(2)}) %collective-permute-start.2) | collective-permute-done | bytes 131104 | tf_op jit(solution)/shard_map/ppermute | solution.py:271
  23.0 0.0 copy-start.3
  23.0 0.0 copy-done.1
  23.0 0.0 copy-done.2
  23.0 0.6 copy-done.3
  23.7 5.1 %shard_map.146 = (f32[1,128]{1,0:T(1,128)}, bf16[8,4,72,128]{3,2,1,0:T(8,128)(2,1)}, f32[4,176,512]{2,1,0:T(8,128)}, bf16[4,176,512]{2,1,0:T(8,128)(2,1)}) custom-call(s32[2]{0:T(128)} %pad_add_fusion.spot_ref, bf16[2,128,256]{2,1,0:T(8,128)(2,1)} %get-tuple-element.21.pick_ref, f32[128,1024]{1,0:T(8,128)} %get-tuple-element.22.q_ref, ...), custom_call_target="tpu_custom_call" | custom-call | tf_op jit(solution)/shard_map/pallas_call | solution.py:29
  28.7 0.6 collective-permute-start.3
  29.4 2.0 %collective-permute-done.3 = bf16[4,176,512]{2,1,0:T(8,128)(2,1)S(1)} collective-permute-done((bf16[4,176,512]{2,1,0:T(8,128)(2,1)}, bf16[4,176,512]{2,1,0:T(8,128)(2,1)S(1)}, u32[]{:S(2)}, u32[]{:S(2)}) %collective-permute-start.3) | collective-permute-done | bytes 720928 | tf_op jit(solution)/shard_map/ppermute | solution.py:307
  31.4 1.5 %add_convert_fusion.3 = (bf16[1,176,512]{2,1,0:T(8,128)(2,1)S(1)}, bf16[176,512]{1,0:T(8,128)(2,1)S(1)}, bf16[176,512]{1,0:T(8,128)(2,1)S(1)}, bf16[176,512]{1,0:T(8,128)(2,1)S(1)}) fusion(f32[4,176,512]{2,1,0:T(8,128)} %get-tuple-element.33, s32[]{:T(128)S(6)} %select_n.25, bf16[4,176,512]{2,1,0:T(8,128)(2,1)S(1)} %collective-permute-done.3, ...), kind=kLoop, calls=%fused_computation.9 | loop fusion | flops 1081344 | bytes 2883600 | tf_op jit(solution)/shard_map/convert_element_type | solution.py:317
  32.9 1.8 %collective-permute-start.6 = (bf16[176,512]{1,0:T(8,128)(2,1)S(1)}, bf16[176,512]{1,0:T(8,128)(2,1)S(1)}, u32[]{:S(2)}, u32[]{:S(2)}) collective-permute-start(bf16[176,512]{1,0:T(8,128)(2,1)S(1)} %get-tuple-element.36), channel_id=1, source_target_pairs={{0,6},{2,4},{4,2},{6,0},{1,7},{3,5},{5,3},{7,1},{8,14},{10,12},{12... | collective-permute-start | bytes 540680 | tf_op jit(solution)/shard_map/ppermute | solution.py:319
  34.7 0.5 collective-permute-start.5
  35.2 1.2 %collective-permute-start.4 = (bf16[176,512]{1,0:T(8,128)(2,1)S(1)}, bf16[176,512]{1,0:T(8,128)(2,1)S(1)}, u32[]{:S(2)}, u32[]{:S(2)}) collective-permute-start(bf16[176,512]{1,0:T(8,128)(2,1)S(1)} %get-tuple-element.38), channel_id=1, source_target_pairs={{0,2},{2,0},{4,6},{6,4},{1,3},{3,1},{5,7},{7,5},{8,10},{10,8},{12,... | collective-permute-start | bytes 540680 | tf_op jit(solution)/shard_map/ppermute | solution.py:319
  36.5 4.9 %collective-permute-done.6 = bf16[176,512]{1,0:T(8,128)(2,1)S(1)} collective-permute-done((bf16[176,512]{1,0:T(8,128)(2,1)S(1)}, bf16[176,512]{1,0:T(8,128)(2,1)S(1)}, u32[]{:S(2)}, u32[]{:S(2)}) %collective-permute-start.6) | collective-permute-done | bytes 180256 | tf_op jit(solution)/shard_map/ppermute | solution.py:319
  41.4 3.2 %collective-permute-done.5 = bf16[176,512]{1,0:T(8,128)(2,1)S(1)} collective-permute-done((bf16[176,512]{1,0:T(8,128)(2,1)S(1)}, bf16[176,512]{1,0:T(8,128)(2,1)S(1)}, u32[]{:S(2)}, u32[]{:S(2)}) %collective-permute-start.5) | collective-permute-done | bytes 180256 | tf_op jit(solution)/shard_map/ppermute | solution.py:319
  44.6 0.1 collective-permute-done.4
  44.7 0.1 fusion.1
  44.8 1.6 %collective-permute-start.7 = (bf16[160,512]{1,0:T(8,128)(2,1)S(1)}, bf16[160,512]{1,0:T(8,128)(2,1)S(1)}, u32[]{:S(2)}, u32[]{:S(2)}) collective-permute-start(bf16[160,512]{1,0:T(8,128)(2,1)S(1)} %fusion.1), channel_id=1, source_target_pairs={{0,8},{8,0},{16,24},{24,16},{1,9},{9,1},{17,25},{25,17},{2,10},{10... | collective-permute-start | bytes 491528 | tf_op jit(solution)/shard_map/ppermute | solution.py:329
  46.4 4.0 %all-to-all-start = ((bf16[32,72,128]{2,1,0:T(8,128)(2,1)}), bf16[32,72,128]{2,1,0:T(8,128)(2,1)S(1)}, u32[]{:S(2)}, u32[]{:S(2)}) async-start(bf16[32,72,128]{2,1,0:T(8,128)(2,1)} %bitcast.9), calls=%async_computation | async-start | bytes 1179648 | tf_op jit(solution)/shard_map/all_to_all | solution.py:309
  50.4 0.4 collective-permute-done.7
  50.9 2.6 %collective-permute-start.8 = (bf16[160,512]{1,0:T(8,128)(2,1)S(1)}, bf16[160,512]{1,0:T(8,128)(2,1)S(1)}, u32[]{:S(2)}, u32[]{:S(2)}) collective-permute-start(bf16[160,512]{1,0:T(8,128)(2,1)S(1)} %add_convert_fusion.5), channel_id=1, source_target_pairs={{0,16},{8,24},{16,0},{24,8},{1,17},{9,25},{17,1},{25,9},{2,18},{10... | collective-permute-start | bytes 491528 | tf_op jit(solution)/shard_map/ppermute | solution.py:329
  53.6 20.3 %collective-permute-done.8 = bf16[160,512]{1,0:T(8,128)(2,1)S(1)} collective-permute-done((bf16[160,512]{1,0:T(8,128)(2,1)S(1)}, bf16[160,512]{1,0:T(8,128)(2,1)S(1)}, u32[]{:S(2)}, u32[]{:S(2)}) %collective-permute-start.8) | collective-permute-done | bytes 163872 | tf_op jit(solution)/shard_map/ppermute | solution.py:329
  73.9 10.5 %all_gather.7 = bf16[640,512]{1,0:T(8,128)(2,1)S(1)} all-gather(bf16[160,512]{1,0:T(8,128)(2,1)S(1)} %add_convert_fusion.4), channel_id=1, replica_groups=mesh['z'=4,'y'=2,'x'=2,'c'=2] {'y','x'}, dimensions={0}, use_global_device_ids=true | all-gather | bytes 819200 | tf_op jit(solution)/shard_map/all_gather | solution.py:341
  84.4 0.0 collective-permute-start.9
  84.4 0.1 collective-permute-start.10
  84.5 3.7 %collective-permute-done.10 = f32[8,512]{1,0:T(8,128)S(1)} collective-permute-done((f32[8,512]{1,0:T(8,128)S(1)}, f32[8,512]{1,0:T(8,128)S(1)}, u32[]{:S(2)}, u32[]{:S(2)}) %collective-permute-start.10) | collective-permute-done | bytes 16416 | tf_op jit(solution)/shard_map/ppermute | solution.py:330
  88.2 0.0 collective-permute-start.11
  88.3 4.6 %collective-permute-done.11 = f32[8,512]{1,0:T(8,128)S(1)} collective-permute-done((f32[8,512]{1,0:T(8,128)S(1)}, f32[8,512]{1,0:T(8,128)S(1)}, u32[]{:S(2)}, u32[]{:S(2)}) %collective-permute-start.11) | collective-permute-done | bytes 16416 | tf_op jit(solution)/shard_map/ppermute | solution.py:330
  92.9 0.6 slice_reduce_fusion
  93.5 0.6 slice_add_fusion.1
  94.1 0.0 all-to-all-done.grads_ref
  94.1 0.0 copy-start
  94.1 0.8 copy-done
  94.9 4.8 %shard_map.147 = f32[2,64,4096]{2,1,0:T(8,128)} custom-call(bf16[32,72,128]{2,1,0:T(8,128)(2,1)} %copy-done), custom_call_target="tpu_custom_call" | custom-call | tf_op jit(solution)/shard_map/pallas_call | solution.py:29
  99.7 0.0 collective-permute-done.9
  99.7 0.1 broadcast_select_fusion.1
  99.8 0.1 slice_bitcast_fusion
  99.9 0.1 pad_maximum_fusion
  100.0 1.7 %bitcast_convert_fusion = f32[1024,512]{1,0:T(8,128)} fusion(bf16[2,512,512]{2,1,0:T(8,128)(2,1)S(1)} %pad_maximum_fusion), kind=kLoop, calls=%fused_computation.1 | loop fusion | flops 524288 | bytes 3145728 | tf_op jit(solution)/shard_map/convert_element_type | solution.py:344
  101.7 0.8 maximum_convert_fusion
  (7 shorter events, 0.1 us)
Async XLA Ops:
  8.6 8.9 %copy-start.4 = (bf16[512]{0:T(512)(128)(2,1)S(1)}, bf16[512]{0:T(512)(128)(2,1)}, u32[]{:S(2)}) copy-start(bf16[512]{0:T(512)(128)(2,1)} %param.16) | copy-start | bytes 3076
  14.8 6.5 %collective-permute-start = (bf16[128,512]{1,0:T(8,128)(2,1)}, bf16[128,512]{1,0:T(8,128)(2,1)S(1)}, u32[]{:S(2)}, u32[]{:S(2)}) collective-permute-start(bf16[128,512]{1,0:T(8,128)(2,1)} %get-tuple-element.26), channel_id=1, source_target_pairs={{0,1},{1,0},{2,3},{3,2},{4,5},{5,4},{6,7},{7,6},{8,9},{9,8},{10,11... | collective-permute-start | bytes 393224 | tf_op jit(solution)/shard_map/ppermute | solution.py:271
  15.2 6.6 %collective-permute-start.1 = (bf16[128,512]{1,0:T(8,128)(2,1)}, bf16[128,512]{1,0:T(8,128)(2,1)S(1)}, u32[]{:S(2)}, u32[]{:S(2)}) collective-permute-start(bf16[128,512]{1,0:T(8,128)(2,1)} %get-tuple-element.27), channel_id=1, source_target_pairs={{0,2},{1,3},{2,0},{3,1},{4,6},{5,7},{6,4},{7,5},{8,10},{9,11},{10,... | collective-permute-start | bytes 393224 | tf_op jit(solution)/shard_map/ppermute | solution.py:271
  16.0 7.0 %collective-permute-start.2 = (bf16[128,512]{1,0:T(8,128)(2,1)}, bf16[128,512]{1,0:T(8,128)(2,1)S(1)}, u32[]{:S(2)}, u32[]{:S(2)}) collective-permute-start(bf16[128,512]{1,0:T(8,128)(2,1)} %get-tuple-element.28), channel_id=1, source_target_pairs={{0,3},{1,2},{2,1},{3,0},{4,7},{5,6},{6,5},{7,4},{8,11},{9,10},{10,... | collective-permute-start | bytes 393224 | tf_op jit(solution)/shard_map/ppermute | solution.py:271
  21.4 1.7 %copy-start.1 = (bf16[128,512]{1,0:T(8,128)(2,1)}, bf16[128,512]{1,0:T(8,128)(2,1)S(1)}, u32[]{:S(2)}) copy-start(bf16[128,512]{1,0:T(8,128)(2,1)S(1)} %collective-permute-done.refs_1_) | copy-start | bytes 393220
  21.8 1.2 %copy-start.2 = (bf16[128,512]{1,0:T(8,128)(2,1)}, bf16[128,512]{1,0:T(8,128)(2,1)S(1)}, u32[]{:S(2)}) copy-start(bf16[128,512]{1,0:T(8,128)(2,1)S(1)} %collective-permute-done.1.refs_2_) | copy-start | bytes 393220
  23.0 0.6 copy-start.3
  28.7 2.7 %collective-permute-start.3 = (bf16[4,176,512]{2,1,0:T(8,128)(2,1)}, bf16[4,176,512]{2,1,0:T(8,128)(2,1)S(1)}, u32[]{:S(2)}, u32[]{:S(2)}) collective-permute-start(bf16[4,176,512]{2,1,0:T(8,128)(2,1)} %get-tuple-element.32), channel_id=1, source_target_pairs={{0,1},{1,0},{2,3},{3,2},{4,5},{5,4},{6,7},{7,6},{8,9},{9,8},{10,11... | collective-permute-start | bytes 2162696 | tf_op jit(solution)/shard_map/ppermute | solution.py:307
  32.9 8.4 %collective-permute-start.6 = (bf16[176,512]{1,0:T(8,128)(2,1)S(1)}, bf16[176,512]{1,0:T(8,128)(2,1)S(1)}, u32[]{:S(2)}, u32[]{:S(2)}) collective-permute-start(bf16[176,512]{1,0:T(8,128)(2,1)S(1)} %get-tuple-element.36), channel_id=1, source_target_pairs={{0,6},{2,4},{4,2},{6,0},{1,7},{3,5},{5,3},{7,1},{8,14},{10,12},{12... | collective-permute-start | bytes 540680 | tf_op jit(solution)/shard_map/ppermute | solution.py:319
  34.7 9.9 %collective-permute-start.5 = (bf16[176,512]{1,0:T(8,128)(2,1)S(1)}, bf16[176,512]{1,0:T(8,128)(2,1)S(1)}, u32[]{:S(2)}, u32[]{:S(2)}) collective-permute-start(bf16[176,512]{1,0:T(8,128)(2,1)S(1)} %get-tuple-element.37), channel_id=1, source_target_pairs={{0,4},{2,6},{4,0},{6,2},{1,5},{3,7},{5,1},{7,3},{8,12},{10,14},{12... | collective-permute-start | bytes 540680 | tf_op jit(solution)/shard_map/ppermute | solution.py:319
  35.2 9.4 %collective-permute-start.4 = (bf16[176,512]{1,0:T(8,128)(2,1)S(1)}, bf16[176,512]{1,0:T(8,128)(2,1)S(1)}, u32[]{:S(2)}, u32[]{:S(2)}) collective-permute-start(bf16[176,512]{1,0:T(8,128)(2,1)S(1)} %get-tuple-element.38), channel_id=1, source_target_pairs={{0,2},{2,0},{4,6},{6,4},{1,3},{3,1},{5,7},{7,5},{8,10},{10,8},{12,... | collective-permute-start | bytes 540680 | tf_op jit(solution)/shard_map/ppermute | solution.py:319
  44.8 6.1 %collective-permute-start.7 = (bf16[160,512]{1,0:T(8,128)(2,1)S(1)}, bf16[160,512]{1,0:T(8,128)(2,1)S(1)}, u32[]{:S(2)}, u32[]{:S(2)}) collective-permute-start(bf16[160,512]{1,0:T(8,128)(2,1)S(1)} %fusion.1), channel_id=1, source_target_pairs={{0,8},{8,0},{16,24},{24,16},{1,9},{9,1},{17,25},{25,17},{2,10},{10... | collective-permute-start | bytes 491528 | tf_op jit(solution)/shard_map/ppermute | solution.py:329
  46.4 47.7 %all-to-all-start = ((bf16[32,72,128]{2,1,0:T(8,128)(2,1)}), bf16[32,72,128]{2,1,0:T(8,128)(2,1)S(1)}, u32[]{:S(2)}, u32[]{:S(2)}) async-start(bf16[32,72,128]{2,1,0:T(8,128)(2,1)} %bitcast.9), calls=%async_computation | async-start | bytes 1179648 | tf_op jit(solution)/shard_map/all_to_all | solution.py:309
  50.9 22.9 %collective-permute-start.8 = (bf16[160,512]{1,0:T(8,128)(2,1)S(1)}, bf16[160,512]{1,0:T(8,128)(2,1)S(1)}, u32[]{:S(2)}, u32[]{:S(2)}) collective-permute-start(bf16[160,512]{1,0:T(8,128)(2,1)S(1)} %add_convert_fusion.5), channel_id=1, source_target_pairs={{0,16},{8,24},{16,0},{24,8},{1,17},{9,25},{17,1},{25,9},{2,18},{10... | collective-permute-start | bytes 491528 | tf_op jit(solution)/shard_map/ppermute | solution.py:329
  84.4 15.3 %collective-permute-start.9 = (bf16[640,512]{1,0:T(8,128)(2,1)S(1)}, bf16[640,512]{1,0:T(8,128)(2,1)S(1)}, u32[]{:S(2)}, u32[]{:S(2)}) collective-permute-start(bf16[640,512]{1,0:T(8,128)(2,1)S(1)} %all_gather.7), channel_id=1, source_target_pairs={{0,1},{1,0},{2,3},{3,2},{4,5},{5,4},{6,7},{7,6},{8,9},{9,8},{10,11... | collective-permute-start | bytes 1966088 | tf_op jit(solution)/shard_map/ppermute | solution.py:342
  84.4 3.8 %collective-permute-start.10 = (f32[8,512]{1,0:T(8,128)S(1)}, f32[8,512]{1,0:T(8,128)S(1)}, u32[]{:S(2)}, u32[]{:S(2)}) collective-permute-start(f32[8,512]{1,0:T(8,128)S(1)} %slice_add_fusion), channel_id=1, source_target_pairs={{0,8},{8,0},{16,24},{24,16},{1,9},{9,1},{17,25},{25,17},{2,10},{10... | collective-permute-start | bytes 49160 | tf_op jit(solution)/shard_map/ppermute | solution.py:330
  88.2 4.6 %collective-permute-start.11 = (f32[8,512]{1,0:T(8,128)S(1)}, f32[8,512]{1,0:T(8,128)S(1)}, u32[]{:S(2)}, u32[]{:S(2)}) collective-permute-start(f32[8,512]{1,0:T(8,128)S(1)} %fusion.6), channel_id=1, source_target_pairs={{0,16},{8,24},{16,0},{24,8},{1,17},{9,25},{17,1},{25,9},{2,18},{10... | collective-permute-start | bytes 49160 | tf_op jit(solution)/shard_map/ppermute | solution.py:330
  94.1 0.8 copy-start
